TPU v7x, 512 devices: a whole 4x4x16 slice. The times are simulated.
512 devices in a mesh: ep: 128 (over x, z, core), dp: 4 (over y).
Axes of the slice: x: 4, y: 4, z: 16, core: 2. Of those that a mesh axis runs over, the one named last changes fastest.
Arguments:
- tokens: bfloat16 [2048, 3584], P('ep'), may hold values from -6 to 6
- expert_ids: int32 [2048, 8], P('ep'), may hold values from 0 to 127, all different within a row; in each aligned block of 16 rows (0 to 15, 16 to 31, ...) at most 4 rows name the same one
- route_logits: float32 [2048, 8], P('ep'), may hold values from -8 to 8
- expert_gate: bfloat16 [128, 3584, 1024], P('ep', None, 'dp'), may hold values from -0.09375 to 0.09375
- expert_up: bfloat16 [128, 3584, 1024], P('ep', None, 'dp'), may hold values from -0.09375 to 0.09375
- expert_down: bfloat16 [128, 1024, 3584], P('ep', 'dp'), may hold values from -0.1875 to 0.1875
Outputs:
- mixed: bfloat16 [2048, 3584], P(('ep', 'dp'))
Inputs may be any that keep to these rules, and one draw needn't show every extreme that they name: `expert_ids`: each row names 8 different experts of 0 to 127 and every expert is named by some row. Within the rows of one index of ep (aligned blocks of 16 rows) no expert is named more than 4 times, and some block names one expert exactly 4 times. Loads are heavy-tailed: a few experts take several times the mean.
All inputs are finite; a program needn't handle non-finite values.
Results may differ from a plain program's by a relative error of at most 0.015.
Values may be sent and summed in bfloat16 or wider, within the bound.
A program may use at most 64 MiB of HBM per device.

v0:
```python
import jax
import jax.numpy as jnp
from jax import lax
from jax.sharding import PartitionSpec as P

route_scale = 2.5


def on_device(tokens, expert_ids, route_logits, expert_gate, expert_up, expert_down):
    tok_rows, width = tokens.shape
    top = expert_ids.shape[1]
    n_ep = lax.axis_size("ep")
    n_dp = lax.axis_size("dp")
    experts = n_ep
    capacity = min(tok_rows, 4 * max(1, tok_rows * top // experts))
    flat_ids = expert_ids.reshape(-1).astype(jnp.int32)
    onehot = (flat_ids[:, None] == jnp.arange(experts, dtype=jnp.int32)[None, :]).astype(jnp.int32)
    earlier = jnp.cumsum(onehot, axis=0).astype(jnp.int32) - onehot
    within = jnp.sum(earlier * onehot, axis=1).astype(jnp.int32)
    slot_index = flat_ids * capacity + within
    token_of_slot = jnp.arange(tok_rows * top, dtype=jnp.int32) // top
    source_row = (
        jnp.full((experts * capacity,), tok_rows, jnp.int32).at[slot_index].set(token_of_slot)
    )
    extended = jnp.concatenate([tokens, jnp.zeros((1, width), tokens.dtype)], axis=0)
    outgoing = extended[source_row].reshape(n_ep, capacity, width)
    arrived = lax.all_to_all(outgoing, "ep", split_axis=0, concat_axis=0, tiled=True)
    received = arrived.reshape(n_ep * capacity, width)
    gate = jnp.dot(received, expert_gate[0], preferred_element_type=jnp.float32)
    upper = jnp.dot(received, expert_up[0], preferred_element_type=jnp.float32)
    hidden = (jax.nn.silu(gate) * upper).astype(jnp.bfloat16)
    partial_value = jnp.dot(hidden, expert_down[0], preferred_element_type=jnp.float32)
    partial_value = partial_value.reshape(n_ep, capacity, width)
    scores = jax.nn.sigmoid(route_logits)
    weights = route_scale * scores / jnp.sum(scores, axis=1, keepdims=True)
    member = lax.axis_index("dp")
    quarter = capacity // n_dp
    reduced = (
        lax.psum_scatter(partial_value.astype(jnp.bfloat16), "dp", scatter_dimension=1, tiled=True)
        .astype(jnp.float32)
        .astype(jnp.bfloat16)
    )
    back = lax.all_to_all(reduced, "ep", split_axis=0, concat_axis=0, tiled=True)
    offset = within - member * quarter
    held = ((offset >= 0) & (offset < quarter)).astype(jnp.float32)
    picked = flat_ids * quarter + jnp.clip(offset, 0, quarter - 1)
    values = back.reshape(experts * quarter, width)[picked].reshape(tok_rows, top, width)
    masked = weights * held.reshape(tok_rows, top)
    contrib = jnp.sum(masked[:, :, None] * values.astype(jnp.float32), axis=1)
    routed = lax.psum_scatter(
        contrib.astype(jnp.bfloat16), "dp", scatter_dimension=0, tiled=True
    ).astype(jnp.float32)
    return routed.astype(jnp.bfloat16)


def solution(mesh):
    placed = (
        P("ep", None),
        P("ep", None),
        P("ep", None),
        P("ep", None, "dp"),
        P("ep", None, "dp"),
        P("ep", "dp", None),
    )
    return jax.shard_map(
        on_device, mesh=mesh, in_specs=placed, out_specs=P(("ep", "dp"), None), check_vma=False
    )
```

profile of v0, /device:TPU:1, one launch (start us, length us, event | category | flops | bytes accessed | tf_op | source)
XLA Modules:
  0.0 400.9 jit_solution(13666367632085230634)
XLA Ops:
  6.5 0.9 copy.20
  8.1 1.0 scatter_custom_fusion
  9.1 0.9 concatenate.3
  10.0 4.2 %gather_fusion = bf16[512,3584]{1,0:T(8,128)(2,1)} fusion(bf16[17,3584]{1,0:T(8,128)(2,1)S(1)} %concatenate.3, s32[1024]{0:T(1024)S(1)} %pad_clamp_fusion.1), kind=kCustom, calls=%fused_computation | custom fusion | bytes 7342080 | tf_op jit(solution)/shard_map/gather | solution.py:26
  14.2 7.0 %reshape.88 = bf16[128,4,3584]{2,1,0:T(4,128)(2,1)} reshape(bf16[512,3584]{1,0:T(8,128)(2,1)} %gather_fusion) | data formatting | bytes 7340032 | tf_op jit(solution)/shard_map/reshape | solution.py:26
  21.2 190.3 %all_to_all.10 = bf16[128,4,3584]{2,1,0:T(4,128)(2,1)} all-to-all(bf16[128,4,3584]{2,1,0:T(4,128)(2,1)} %reshape.88), channel_id=1, replica_groups=mesh['ep'=128,'dp'=4] {'ep'}, dimensions={0} | all-to-all | bytes 7340032 | tf_op jit(solution)/shard_map/all_to_all | solution.py:27
  211.5 6.7 %reshape.89 = bf16[512,3584]{1,0:T(8,128)(2,1)} reshape(bf16[128,4,3584]{2,1,0:T(4,128)(2,1)} %all_to_all.10) | data formatting | bytes 7340032 | tf_op jit(solution)/shard_map/reshape | solution.py:28
  218.2 3.9 fusion.4
  222.1 0.4 copy-done.3
  222.5 1.1 fusion.9
  223.7 2.9 convolution_convert_fusion
  226.6 41.8 %reduce-scatter.2.cloned.1.call-done = bf16[128,1,3584]{2,0,1:T(8,128)(2,1)} async-done(((bf16[128,4,3584]{2,0,1:T(8,128)(2,1)}), bf16[128,1,3584]{2,0,1:T(8,128)(2,1)}) %reduce-scatter.2.cloned.1.call-update) | async-done | bytes 917520 | tf_op jit(solution)/shard_map/reduce_scatter | solution.py:39
  268.4 0.5 broadcast.120
  268.9 2.5 reduce
  271.4 1.1 reshape.121
  272.6 16.9 %all-to-all-start.1 = ((bf16[128,2,1792]{2,1,0:T(2,128)(2,1)}), bf16[128,2,1792]{2,1,0:T(2,128)(2,1)S(1)}, u32[]{:S(2)}, u32[]{:S(2)}) async-start(bf16[128,2,1792]{2,1,0:T(2,128)(2,1)} %reshape.121), calls=%async_computation.2 | async-start | bytes 1835008 | tf_op jit(solution)/shard_map/all_to_all | solution.py:43
  289.9 49.9 %all-to-all-done.1 = bf16[128,2,1792]{2,1,0:T(2,128)(2,1)S(1)} async-done(((bf16[128,2,1792]{2,1,0:T(2,128)(2,1)}), bf16[128,2,1792]{2,1,0:T(2,128)(2,1)S(1)}, u32[]{:S(2)}, u32[]{:S(2)}) %all-to-all-start.1) | async-done | bytes 917536 | tf_op jit(solution)/shard_map/all_to_all | solution.py:43
  339.8 2.1 reshape.122
  341.9 1.6 copy.29
  343.5 2.0 gather_fusion.1
  345.6 2.5 fusion
  348.1 1.3 dynamic-slice
  350.1 42.6 %all-reduce.4.cloned.1.call-done = bf16[16,3584]{1,0:T(8,128)(2,1)} async-done(((bf16[16,3584]{1,0:T(8,128)(2,1)}), bf16[16,3584]{1,0:T(8,128)(2,1)}) %all-reduce.4.cloned.1.call-update) | async-done | bytes 114704
  392.6 1.4 constant_dynamic-slice_fusion
  (27 shorter events, 1.1 us)
Async XLA Ops:
  6.5 217.1 %copy-start = (bf16[1,256,3584]{2,1,0:T(8,128)(2,1)S(1)}, bf16[1,256,3584]{2,1,0:T(8,128)(2,1)}, u32[]{:S(2)}) copy-start(bf16[1,256,3584]{2,1,0:T(8,128)(2,1)} %param.11) | copy-start | bytes 5505028
  6.5 261.9 %reduce-scatter.2.cloned.1.call-start = ((), (), s32[]{:S(2)}) async-start(), calls=%async_computation.3 | async-start | bytes 4587520 | tf_op jit(solution)/shard_map/reduce_scatter | solution.py:39
  218.2 3.9 copy-start.1
  218.2 4.3 %copy-start.3 = (bf16[1,3584,256]{2,1,0:T(8,128)(2,1)S(1)}, bf16[1,3584,256]{2,1,0:T(8,128)(2,1)}, u32[]{:S(2)}) copy-start(bf16[1,3584,256]{2,1,0:T(8,128)(2,1)} %param.10) | copy-start | bytes 5505028
  226.6 63.0 %copy-start.2 = (f32[16,8]{0,1:T(8,128)S(1)}, f32[16,8]{0,1:T(8,128)}, u32[]{:S(2)}) copy-start(f32[16,8]{0,1:T(8,128)} %param.8) | copy-start | bytes 1540
  272.6 67.2 %all-to-all-start.1 = ((bf16[128,2,1792]{2,1,0:T(2,128)(2,1)}), bf16[128,2,1792]{2,1,0:T(2,128)(2,1)S(1)}, u32[]{:S(2)}, u32[]{:S(2)}) async-start(bf16[128,2,1792]{2,1,0:T(2,128)(2,1)} %reshape.121), calls=%async_computation.2 | async-start | bytes 1835008 | tf_op jit(solution)/shard_map/all_to_all | solution.py:43
  289.5 103.2 %all-reduce.4.cloned.1.call-start = ((), (), s32[]{:S(2)}) async-start(), calls=%async_computation.4 | async-start | bytes 229376
Sparse Core Ops, SparseCore 0:
  226.7 41.6 reduce-scatter.1
  348.3 44.3 all-reduce.3
where the time goes:
time: 403 us; the launch traced here: 401 us
  blocking collectives  190 us (47%)
  waiting for transfers between devices  134 us (33%)
  local copies, waits for them, and re-layouts  31.7 us (8%)
  starting transfers between devices  16.9 us (4%)
  between operations  14.2 us (4%)
  matrix products  7.88 us (2%)
  other arithmetic  5.68 us (1%)
    all_to_all x1, blocking collectives, on_device(): lax.all_to_all(outgoing, 'ep', split_axis=0, concat_axis=0, tiled=True)  190 us
    all_to_all x1, waiting for transfers between devices, on_device(): lax.all_to_all(reduced, 'ep', split_axis=0, concat_axis=0, tiled=True)  49.9 us
    unnamed x3, waiting for transfers between devices  42.6 us
    reduce_scatter x1, waiting for transfers between devices, on_device(): lax.psum_scatter(partial_value.astype(jnp.bfloat16), 'dp', scatter_dimens...  41.8 us
    all_to_all x1, starting transfers between devices, on_device(): lax.all_to_all(reduced, 'ep', split_axis=0, concat_axis=0, tiled=True)  16.9 us
    unnamed x15, local copies, waits for them, and re-layouts  8.92 us
  transfers between devices with their start and end apart: 3, of which 3 were waited for; matrix products, arithmetic and copies ran while one was open for 0% of the time, Pallas kernels for 0%

commit v1 on v0

v1 whole, which is shorter than its diff:
```python
import functools

import jax
import jax.numpy as jnp
from jax import lax
from jax.experimental import pallas as pl
from jax.experimental.pallas import tpu as pltpu
from jax.sharding import PartitionSpec as P

MESH = pl.DeviceIdType.MESH
F32 = jnp.float32
BF16 = jnp.bfloat16
ROUTE_SCALE = 2.5
CAP = 4
CHIPS_X = 4
CORES = 2
N_DP = 4


def kernel(
    nx, nz, ids_ref, logits_ref, tok_ref, wg_hbm, wu_hbm, wd_hbm, out_ref,
    wg, wu, wd, zbuf, swbuf, xsend, ybuf, obuf, r1buf, r2buf, xret, rbuf, part,
    zs1, zs2, zr1, zr2, fbuf,
    w_sem, zag_s, zag_r, x_s, x_r, y1_s, y1_r, y2_s, y2_r, p1_s, p1_r, p2_s, p2_r,
    b_s, b_r, zrs_s, zrs_r, f_s, f_r,
):
    nc, ny = CORES, N_DP
    tile = tok_ref.shape[0]
    width = tok_ref.shape[1]
    quarter = width // ny
    top = ids_ref.shape[1]
    col = nz * tile
    slots = nz * CAP
    group = nc * slots
    half = group // 2
    offsets = {1: (0,), 2: (0, 1), 4: (0, 1, 3, 2)}[nx]
    inverse = [offsets.index((nx - o) % nx) for o in offsets]
    ep = lax.axis_index("ep")
    y = lax.axis_index("dp")
    c = lax.rem(ep, nc)
    z = lax.rem(lax.div(ep, nc), nz)
    x = lax.div(ep, nc * nz)

    def dev(x_, y_, z_, c_):
        return (((x_ * nz + z_) * nc + c_), y_)

    def at_x(r):
        return lax.rem(x + offsets[r], nx)

    def at_y(o):
        return lax.rem(y + (o + ny), ny)

    def at_z(o):
        return lax.rem(z + (o + 2 * nz), nz)

    def rows(start, size):
        if isinstance(start, int):
            return pl.ds(start, size)
        return pl.ds(pl.multiple_of(start, size), size)

    sends = []

    def send(src, dst, ssem, rsem, device):
        copy = pltpu.make_async_remote_copy(
            src_ref=src, dst_ref=dst, send_sem=ssem, recv_sem=rsem,
            device_id=device, device_id_type=MESH,
        )
        copy.start()
        sends.append(copy)
        return copy

    def arrived(ref, rsem):
        pltpu.make_async_remote_copy(
            src_ref=ref, dst_ref=ref, send_sem=rsem, recv_sem=rsem,
            device_id=dev(x, y, z, 1 - c), device_id_type=MESH,
        ).wait_recv()

    loads = [
        pltpu.make_async_copy(s.at[0], d, w_sem.at[i])
        for i, (s, d) in enumerate(((wg_hbm, wg), (wu_hbm, wu), (wd_hbm, wd)))
    ]
    for load in loads:
        load.start()

    scores = 1.0 / (1.0 + jnp.exp(-logits_ref[...]))
    wts = ROUTE_SCALE * scores / jnp.sum(scores, axis=1, keepdims=True)
    lane = lax.broadcasted_iota(jnp.int32, (top, 128), 1)
    sub = lax.broadcasted_iota(jnp.int32, (top, 128), 0)
    put_id = (lane == sub).astype(BF16)
    put_w = (lane == sub + top).astype(BF16)
    meta = jnp.dot(
        ids_ref[...].astype(F32).astype(BF16), put_id, preferred_element_type=F32
    ) + jnp.dot(wts.astype(BF16), put_w, preferred_element_type=F32)
    own = rows(z * tile, tile)
    zbuf[own, 0:quarter] = tok_ref[:, pl.ds(pl.multiple_of(y * quarter, 128), quarter)]
    zbuf[own, quarter : quarter + 128] = meta.astype(BF16)

    barrier = pltpu.get_barrier_semaphore()
    peers = [dev(x, y, at_z(o), c) for o in (1, -1, 2, -2)]
    peers += [dev(at_x(r), y, z, c_) for r in range(1, nx) for c_ in range(nc)]
    peers += [dev(x, y, z, 1 - c)]
    peers += [dev(x, at_y(o), z, c) for o in range(1, ny)]
    for peer in peers:
        pl.semaphore_signal(barrier, inc=1, device_id=peer, device_id_type=MESH)
    pl.semaphore_wait(barrier, len(peers))

    steps = nz // 4

    def zsem(d, k, hop):
        return ((0 if d > 0 else 1) * steps + (k - 1)) * 2 + (hop - 1)

    def zblock(o):
        return zbuf.at[rows(at_z(o) * tile, tile), :]

    pending = {}
    for k in range(1, steps + 1):
        for d in (1, -1):
            if k > 1:
                pending.pop((d, k - 1, 2)).wait_recv()
            for hop in (1, 2):
                if hop == 2 and d < 0 and k == steps:
                    continue
                block = zblock(-d * 2 * (k - 1))
                i = zsem(d, k, hop)
                pending[(d, k, hop)] = send(
                    block, block, zag_s.at[i], zag_r.at[i], dev(x, y, at_z(d * hop), c)
                )
    for copy in pending.values():
        copy.wait_recv()

    pick = (
        lax.broadcasted_iota(jnp.int32, (2 * top, 128), 0)
        == lax.broadcasted_iota(jnp.int32, (2 * top, 128), 1)
    ).astype(BF16)
    by_token = lax.dot_general(
        pick, zbuf[:, quarter : quarter + 128], (((1,), (1,)), ((), ())),
        preferred_element_type=F32,
    )
    lanes = nx * nc
    j = lax.broadcasted_iota(jnp.int32, (lanes, col), 0)
    jr, jc = lax.div(j, nc), lax.rem(j, nc)
    off = jnp.zeros_like(jr)
    for r, o in enumerate(offsets):
        off = jnp.where(jr == r, o, off)
    expert = ((lax.rem(x + off, nx) * nz + z) * nc + jc).astype(F32)
    named = jnp.zeros((lanes, col), F32)
    weight = jnp.zeros((lanes, col), F32)
    for k in range(top):
        hit = by_token[k : k + 1, :] == expert
        named = jnp.where(hit, 1.0, named)
        weight = jnp.where(hit, by_token[top + k : top + k + 1, :], weight)
    t_row = lax.broadcasted_iota(jnp.int32, (col, col), 0)
    t_col = lax.broadcasted_iota(jnp.int32, (col, col), 1)
    before = ((t_row < t_col) & (lax.div(t_row, tile) == lax.div(t_col, tile))).astype(BF16)
    rank = jnp.dot(named.astype(BF16), before, preferred_element_type=F32)
    rank = jnp.where(named > 0.5, rank, -1.0)
    s_row = lax.broadcasted_iota(jnp.int32, (slots, col), 0)
    s_col = lax.broadcasted_iota(jnp.int32, (slots, col), 1)
    in_block = lax.div(s_row, CAP) == lax.div(s_col, tile)
    want = jnp.where(in_block, lax.rem(s_row, CAP).astype(F32), -2.0)

    for r in tuple(range(nx - 1, 0, -1)) + (0,):
        chosen = []
        for c_ in range(nc):
            i = r * nc + c_
            hit = rank[i : i + 1, :] == want
            chosen.append(jnp.where(hit, 1.0, 0.0).astype(BF16))
            swbuf[rows(i * slots, slots), :] = jnp.where(hit, weight[i : i + 1, :], 0.0).astype(BF16)
        base = r * group
        xsend[rows(base, group), :] = jnp.dot(
            jnp.concatenate(chosen, axis=0), zbuf[:, 0:quarter], preferred_element_type=F32
        ).astype(BF16)
        land = ybuf.at[y, rows((inverse[r] * nc + c) * slots, slots), :]
        if r > 0:
            for c_ in range(nc):
                i = r * nc + c_
                send(
                    xsend.at[rows(i * slots, slots), :], land, x_s.at[i],
                    x_r.at[inverse[r] * nc + c], dev(at_x(r), y, z, c_),
                )
        else:
            other = 1 - c
            send(
                xsend.at[rows(other * slots, slots), :], land, x_s.at[0], x_r.at[c],
                dev(x, y, z, other),
            )
            ybuf[y, rows(c * slots, slots), :] = xsend[rows(c * slots, slots), :]

    y_one, y_two, p_one, p_two = {}, {}, {}, {}
    for g in range(nx):
        if g == 0:
            arrived(ybuf.at[y, rows((1 - c) * slots, slots), :], x_r.at[1 - c])
        else:
            for c_ in range(nc):
                i = g * nc + c_
                arrived(ybuf.at[y, rows(i * slots, slots), :], x_r.at[i])
        block = ybuf.at[y, rows(g * group, group), :]
        for n, d in enumerate((1, -1)):
            y_one[g, d] = send(
                block, block, y1_s.at[n * nx + g], y1_r.at[n * nx + g], dev(x, at_y(d), z, c)
            )

    def forward(g):
        for n, d in enumerate((1, -1)):
            y_one[g, d].wait_recv()
        for n, d in enumerate((1, -1)):
            block = ybuf.at[at_y(-d), rows(g * group + n * half, half), :]
            y_two[g, d] = send(
                block, block, y2_s.at[n * nx + g], y2_r.at[n * nx + g], dev(x, at_y(d), z, c)
            )

    def compute(g):
        for d in (1, -1):
            y_two[g, d].wait_recv()
        if g == 0:
            for load in loads:
                load.wait()
        here = rows(g * group, group)
        gate = jnp.zeros((group, wg.shape[1]), F32)
        upper = jnp.zeros((group, wg.shape[1]), F32)
        for q in range(ny):
            piece = ybuf[q, here, :]
            deep = pl.ds(q * quarter, quarter)
            gate += jnp.dot(piece, wg[deep, :], preferred_element_type=F32)
            upper += jnp.dot(piece, wu[deep, :], preferred_element_type=F32)
        hidden = (gate / (1.0 + jnp.exp(-gate)) * upper).astype(BF16)
        for q in range(ny):
            obuf[q, here, :] = jnp.dot(
                hidden, wd[:, q * quarter : (q + 1) * quarter], preferred_element_type=F32
            ).astype(BF16)
        for n, d in enumerate((1, -1)):
            p_one[g, d] = send(
                obuf.at[at_y(2), rows(g * group + n * half, half), :],
                r1buf.at[n, rows(g * half, half), :],
                p1_s.at[n * nx + g], p1_r.at[n * nx + g], dev(x, at_y(d), z, c),
            )

    def reduce_one(g):
        for n, d in enumerate((1, -1)):
            p_one[g, d].wait_recv()
            here = rows(g * group + n * half, half)
            q = at_y(d)
            total = obuf[q, here, :].astype(F32) + r1buf[n, rows(g * half, half), :].astype(F32)
            obuf[q, here, :] = total.astype(BF16)
        for n, d in enumerate((1, -1)):
            p_two[g, d] = send(
                obuf.at[at_y(d), rows(g * group, group), :],
                r2buf.at[n, rows(g * group, group), :],
                p2_s.at[n * nx + g], p2_r.at[n * nx + g], dev(x, at_y(d), z, c),
            )

    def reduce_two(g):
        for d in (1, -1):
            p_two[g, d].wait_recv()
        here = rows(g * group, group)
        total = obuf[y, here, :].astype(F32) + r2buf[0, here, :].astype(F32)
        xret[here, :] = (total + r2buf[1, here, :].astype(F32)).astype(BF16)
        land = rbuf.at[rows((inverse[g] * nc + c) * slots, slots), :]
        if g > 0:
            for c_ in range(nc):
                i = g * nc + c_
                send(
                    xret.at[rows(i * slots, slots), :], land, b_s.at[i],
                    b_r.at[inverse[g] * nc + c], dev(at_x(g), y, z, c_),
                )
        else:
            other = 1 - c
            send(
                xret.at[rows(other * slots, slots), :], land, b_s.at[0], b_r.at[c],
                dev(x, y, z, other),
            )
            rbuf[rows(c * slots, slots), :] = xret[rows(c * slots, slots), :]

    def combine(g):
        r = inverse[g]
        if g == 0:
            arrived(rbuf.at[rows((1 - c) * slots, slots), :], b_r.at[1 - c])
        else:
            for c_ in range(nc):
                i = r * nc + c_
                arrived(rbuf.at[rows(i * slots, slots), :], b_r.at[i])
        here = rows(r * group, group)
        term = lax.dot_general(
            swbuf[here, :], rbuf[here, :], (((0,), (0,)), ((), ())), preferred_element_type=F32
        )
        if g == 0:
            part[...] = term
        else:
            part[...] += term

    stages = (forward, compute, reduce_one, reduce_two, combine)
    for i in range(nx + len(stages) - 1):
        for n, stage in enumerate(stages):
            if 0 <= i - n < nx:
                stage(i - n)

    reach = nz // 2

    def block_of(o):
        return part[rows(at_z(o) * tile, tile), :]

    def zslot(d, k):
        return (0 if d > 0 else 1) * steps + (k - 1)

    got = {}

    def zsend(d, k, hop, value):
        src, dst = (zs1, zr1) if hop == 1 else (zs2, zr2)
        i, n = zsem(d, k, hop), zslot(d, k)
        src[n] = value.astype(BF16)
        got[d, k, hop] = (
            send(src.at[n], dst.at[n], zrs_s.at[i], zrs_r.at[i], dev(x, y, at_z(d * hop), c)), dst, n
        )

    def zget(d, k):
        total = None
        for hop in (1, 2):
            if (d, k, hop) in got:
                copy, dst, n = got[d, k, hop]
                copy.wait_recv()
                value = dst[n].astype(F32)
                total = value if total is None else total + value
        return total

    zsend(1, 1, 2, block_of(reach))
    for k in range(1, steps + 1):
        for d in (1, -1):
            zsend(d, k, 1, block_of(d * (reach + 1 - 2 * k)))
    for k in range(1, steps):
        for d in (1, -1):
            zsend(d, k + 1, 2, block_of(d * (reach - 2 * k)) + zget(d, k))
    final = (block_of(0) + zget(1, steps) + zget(-1, steps)).astype(BF16)

    fbuf[y] = final
    tails = []
    for o in range(1, ny):
        tails.append(
            send(fbuf.at[y], fbuf.at[y], f_s.at[o], f_r.at[o], dev(x, at_y(o), z, c))
        )
    mine = out_ref.shape[0]
    sel = (
        lax.broadcasted_iota(jnp.int32, (8, tile), 1)
        == lax.broadcasted_iota(jnp.int32, (8, tile), 0) + y * mine
    ).astype(BF16)
    for tail in tails:
        tail.wait_recv()
    for q in range(ny):
        full = jnp.dot(sel, fbuf[q], preferred_element_type=F32)
        out_ref[:, q * quarter : (q + 1) * quarter] = full[0:mine, :].astype(BF16)
    for copy in sends:
        copy.wait_send()


def on_device(tokens, expert_ids, route_logits, expert_gate, expert_up, expert_down):
    n_ep, ny = lax.axis_size("ep"), N_DP
    nx, nc = CHIPS_X, CORES
    nz = n_ep // (nx * nc)
    tile, width = tokens.shape
    hidden = expert_gate.shape[2]
    quarter = width // ny
    col, slots = nz * tile, nz * CAP
    every = nx * nc * slots
    steps = nz // 4
    dma = pltpu.SemaphoreType.DMA
    vmem = pl.BlockSpec(memory_space=pltpu.VMEM)
    hbm = pl.BlockSpec(memory_space=pl.ANY)
    flops = 6 * every * width * hidden
    return pl.pallas_call(
        functools.partial(kernel, nx, nz),
        out_shape=jax.ShapeDtypeStruct((tile // ny, width), BF16),
        in_specs=[vmem, vmem, vmem, hbm, hbm, hbm],
        out_specs=vmem,
        scratch_shapes=[
            pltpu.VMEM((width, hidden), BF16),
            pltpu.VMEM((width, hidden), BF16),
            pltpu.VMEM((hidden, width), BF16),
            pltpu.VMEM((col, quarter + 128), BF16),
            pltpu.VMEM((every, col), BF16),
            pltpu.VMEM((every, quarter), BF16),
            pltpu.VMEM((ny, every, quarter), BF16),
            pltpu.VMEM((ny, every, quarter), BF16),
            pltpu.VMEM((2, every // 2, quarter), BF16),
            pltpu.VMEM((2, every, quarter), BF16),
            pltpu.VMEM((every, quarter), BF16),
            pltpu.VMEM((every, quarter), BF16),
            pltpu.VMEM((col, quarter), F32),
            pltpu.VMEM((2 * steps, tile, quarter), BF16),
            pltpu.VMEM((2 * steps, tile, quarter), BF16),
            pltpu.VMEM((2 * steps, tile, quarter), BF16),
            pltpu.VMEM((2 * steps, tile, quarter), BF16),
            pltpu.VMEM((ny, tile, quarter), BF16),
            dma((3,)),
            dma((4 * steps,)), dma((4 * steps,)),
            dma((nx * nc,)), dma((nx * nc,)),
            dma((2 * nx,)), dma((2 * nx,)),
            dma((2 * nx,)), dma((2 * nx,)),
            dma((2 * nx,)), dma((2 * nx,)),
            dma((2 * nx,)), dma((2 * nx,)),
            dma((nx * nc,)), dma((nx * nc,)),
            dma((4 * steps,)), dma((4 * steps,)),
            dma((ny,)), dma((ny,)),
        ],
        compiler_params=pltpu.CompilerParams(
            collective_id=0, has_side_effects=True, vmem_limit_bytes=56 * 1024 * 1024
        ),
        cost_estimate=pl.CostEstimate(flops=flops, bytes_accessed=8 << 20, transcendentals=0),
    )(expert_ids, route_logits, tokens, expert_gate, expert_up, expert_down)


def solution(mesh):
    placed = (
        P("ep", None),
        P("ep", None),
        P("ep", None),
        P("ep", None, "dp"),
        P("ep", None, "dp"),
        P("ep", "dp", None),
    )
    return jax.shard_map(
        on_device, mesh=mesh, in_specs=placed, out_specs=P(("ep", "dp"), None), check_vma=False
    )
```

time: 403 us -> 130 us (0.32)
  blocking collectives: 190 us -> 0 us
  waiting for transfers between devices: 134 us -> 0 us
  Pallas kernels: 0 us -> 125 us
  local copies, waits for them, and re-layouts: 31.7 us -> 4.07 us
  starting transfers between devices: 16.9 us -> 0 us
  between operations: 14.2 us -> 0.01 us
  matrix products: 7.88 us -> 0 us
  other arithmetic: 5.68 us -> 0 us
    all_to_all x1 -> x0, blocking collectives: 190 us -> none  [on_device(): lax.all_to_all(outgoing, 'ep', split_axis=0, concat_axis=0, tiled=True)]
    pallas_call x0 -> x1, Pallas kernels: none -> 125 us  [on_device(): pl.pallas_call(functools.partial(kernel, nx, nz), out_shape=jax.ShapeDtyp...]
    all_to_all x1 -> x0, waiting for transfers between devices: 49.9 us -> none  [on_device(): lax.all_to_all(reduced, 'ep', split_axis=0, concat_axis=0, tiled=True)]
    unnamed x3 -> x0, waiting for transfers between devices: 42.6 us -> none
    reduce_scatter x1 -> x0, waiting for transfers between devices: 41.8 us -> none  [on_device(): lax.psum_scatter(partial_value.astype(jnp.bfloat16), 'dp', scatter_dimens...]
    all_to_all x1 -> x0, starting transfers between devices: 16.9 us -> none  [on_device(): lax.all_to_all(reduced, 'ep', split_axis=0, concat_axis=0, tiled=True)]
    reshape x3 -> x0, local copies, waits for them, and re-layouts: 13.8 us -> none  [the longest x1 7 us: on_device(): outgoing = extended[source_row].reshape(n_ep, capacity, width)]
    dot_general x3 -> x0, matrix products: 7.88 us -> none  [the longest x1 3.86 us: on_device(): gate = jnp.dot(received, expert_gate[0], preferred_element_type=jnp.float32)]
  transfers between devices with their start and end apart: 3 -> 0, of which waited for: 3 -> 0; matrix products, arithmetic and copies ran while one was open for 0% -> 0% of each run, Pallas kernels for 0% -> 0%
where the time goes in v1:
time: 130 us
  Pallas kernels  125 us (96%)
  local copies, waits for them, and re-layouts  4.07 us (3%)
    pallas_call x1, Pallas kernels, on_device(): pl.pallas_call(functools.partial(kernel, nx, nz), out_shape=jax.ShapeDtyp...  125 us
    unnamed x3, local copies, waits for them, and re-layouts  4.07 us

profile of v1, /device:TPU:1, one launch (start us, length us, event | category | flops | bytes accessed | tf_op | source)
XLA Modules:
  0.0 129.6 jit_solution(16974906912747654816)
XLA Ops:
  0.0 1.4 %copy.7.ids_ref = s32[16,8]{1,0:T(8,128)} copy(s32[16,8]{0,1:T(8,128)} %param.7) | data formatting | bytes 1024 | tf_op args[1]
  1.4 1.3 %copy.8.logits_ref = f32[16,8]{1,0:T(8,128)} copy(f32[16,8]{0,1:T(8,128)} %param.8) | data formatting | bytes 1024 | tf_op args[2]
  2.7 125.5 %shard_map.64 = bf16[4,3584]{1,0:T(4,128)(2,1)} custom-call(s32[16,8]{1,0:T(8,128)} %copy.7.ids_ref, f32[16,8]{1,0:T(8,128)} %copy.8.logits_ref, bf16[16,3584]{1,0:T(8,128)(2,1)} %tok_ref.1, bf16[1,3584,256]{2,1,0:T(8,128)(2,1)} %wg_hbm.1, bf16[1,3584,256]{2,1,0:T(8,128)(2,1)} %wu_hbm.1, bf16[1,256,3584]{2,1,0:T(8,128)(2,1)} %wd_hbm.1), custom_call_target="tpu_custom_call" | custom-call | flops 2818572288 | bytes 8388608 | tf_op jit(solution)/shard_map/pallas_call | solution.py:368
  128.2 1.4 %copy.10 = bf16[4,3584]{1,0:T(4,128)(2,1)} copy(bf16[4,3584]{1,0:T(4,128)(2,1)} %shard_map.64) | data formatting | bytes 57344

commit v2 on v1

v2 whole, which is shorter than its diff:
```python
import functools

import jax
import jax.numpy as jnp
from jax import lax
from jax.experimental import pallas as pl
from jax.experimental.pallas import tpu as pltpu
from jax.sharding import PartitionSpec as P

MESH = pl.DeviceIdType.MESH
F32 = jnp.float32
BF16 = jnp.bfloat16
ROUTE_SCALE = 2.5
CAP = 4
CHIPS_X = 4
CORES = 2
N_DP = 4


def kernel(
    nx, nz, ids_ref, logits_ref, tok_hbm, wg_hbm, wu_hbm, wd_hbm, out_ref,
    wg, wu, wd, zbuf, swbuf, xsend, ybuf, obuf, r1buf, r2buf, xret, rbuf, part,
    zs1, zs2, zr1, zr2, fsend, frecv,
    w_sem, zag_s, zag_r, x_s, x_r, y1_s, y1_r, y2_s, y2_r, p1_s, p1_r, p2_s, p2_r,
    b_s, b_r, zrs_s, zrs_r, f_s, f_r,
):
    nc, ny = CORES, N_DP
    tile, width = tok_hbm.shape
    quarter = width // ny
    top = ids_ref.shape[0]
    col = nz * tile // 2
    near_blocks = nz // 2
    slots = near_blocks * CAP
    pair = 2 * nc * slots
    each = nx * nc * slots
    hp = pair // 2
    pairs = nx // 2
    offsets = {2: (0, 1), 4: (0, 1, 3, 2)}[nx]
    ep = lax.axis_index("ep")
    y = lax.axis_index("dp")
    c = lax.rem(ep, nc)
    z = lax.rem(lax.div(ep, nc), nz)
    x = lax.div(ep, nc * nz)

    def dev(x_, y_, z_, c_):
        return (((x_ * nz + z_) * nc + c_), y_)

    def to_x(g):
        return lax.rem(x + (nx - offsets[g]), nx)

    def from_x(g):
        return lax.rem(x + offsets[g], nx)

    def at_y(o):
        return lax.rem(y + (o + ny), ny)

    def at_z(o):
        return lax.rem(z + (o + nz), nz)

    def place(o):
        return ((o + nz // 4) % nz) * tile

    def rows(start, size):
        if isinstance(start, int):
            return pl.ds(start, size)
        return pl.ds(pl.multiple_of(start, size), size)

    def base(h, g, c_):
        return h * each + (g * nc + c_) * slots

    sends = []

    def send(src, dst, ssem, rsem, device):
        copy = pltpu.make_async_remote_copy(
            src_ref=src, dst_ref=dst, send_sem=ssem, recv_sem=rsem,
            device_id=device, device_id_type=MESH,
        )
        copy.start()
        sends.append(copy)
        return copy

    def arrived(ref, rsem):
        pltpu.make_async_remote_copy(
            src_ref=ref, dst_ref=ref, send_sem=rsem, recv_sem=rsem,
            device_id=dev(x, y, z, 1 - c), device_id_type=MESH,
        ).wait_recv()

    own = pl.ds(place(0), tile)
    mine = pltpu.make_async_copy(
        tok_hbm.at[:, pl.ds(pl.multiple_of(y * quarter, 128), quarter)],
        zbuf.at[own, pl.ds(0, quarter)], w_sem.at[3],
    )
    mine.start()
    scores = 1.0 / (1.0 + jnp.exp(-logits_ref[...]))
    wts = ROUTE_SCALE * scores / jnp.sum(scores, axis=0, keepdims=True)
    lane = lax.broadcasted_iota(jnp.int32, (top, 128), 1)
    sub = lax.broadcasted_iota(jnp.int32, (top, 128), 0)
    put_id = (lane == sub).astype(BF16)
    put_w = (lane == sub + top).astype(BF16)
    across = (((0,), (0,)), ((), ()))
    meta = lax.dot_general(
        ids_ref[...].astype(F32).astype(BF16), put_id, across, preferred_element_type=F32
    ) + lax.dot_general(wts.astype(BF16), put_w, across, preferred_element_type=F32)
    zbuf[own, quarter : quarter + 128] = meta.astype(BF16)

    barrier = pltpu.get_barrier_semaphore()
    peers = [dev(x, y, at_z(o), c) for o in (1, -1, 2, -2)]
    peers += [dev(from_x(g), y, z, c_) for g in range(1, nx) for c_ in range(nc)]
    peers += [dev(x, y, z, 1 - c)]
    peers += [dev(x, at_y(o), z, c) for o in range(1, ny)]
    for peer in peers:
        pl.semaphore_signal(barrier, inc=1, device_id=peer, device_id_type=MESH)

    loads = [
        pltpu.make_async_copy(s.at[0], d, w_sem.at[i])
        for i, (s, d) in enumerate(((wg_hbm, wg), (wu_hbm, wu), (wd_hbm, wd)))
    ]
    for load in loads:
        load.start()
    mine.wait()
    pl.semaphore_wait(barrier, len(peers))

    steps = nz // 4

    def zsem(d, k, hop):
        return ((0 if d > 0 else 1) * steps + (k - 1)) * 2 + (hop - 1)

    gathers = {}

    def gather_send(k, d):
        o = -d * 2 * (k - 1)
        for hop in (2, 1):
            if hop == 2 and d < 0 and k == steps:
                continue
            i = zsem(d, k, hop)
            gathers[k, d, hop] = send(
                zbuf.at[pl.ds(place(o), tile), :], zbuf.at[pl.ds(place(o - d * hop), tile), :],
                zag_s.at[i], zag_r.at[i], dev(x, y, at_z(d * hop), c),
            )

    def gather_wait(k, d, hop):
        if (k, d, hop) in gathers:
            gathers.pop((k, d, hop)).wait_recv()

    def gather_step(k):
        for d in (1, -1):
            gather_wait(k, d, 2)
            if k < steps:
                gather_send(k + 1, d)

    def routes(h):
        pick = (
            lax.broadcasted_iota(jnp.int32, (2 * top, 128), 0)
            == lax.broadcasted_iota(jnp.int32, (2 * top, 128), 1)
        ).astype(BF16)
        by_token = lax.dot_general(
            pick, zbuf[h * col : (h + 1) * col, quarter : quarter + 128],
            (((1,), (1,)), ((), ())), preferred_element_type=F32,
        )
        lanes = nx * nc
        j = lax.broadcasted_iota(jnp.int32, (lanes, col), 0)
        jg, jc = lax.div(j, nc), lax.rem(j, nc)
        off = jnp.zeros_like(jg)
        for g, o in enumerate(offsets):
            off = jnp.where(jg == g, nx - o, off)
        expert = ((lax.rem(x + off, nx) * nz + z) * nc + jc).astype(F32)
        named = jnp.zeros((lanes, col), F32)
        weight = jnp.zeros((lanes, col), F32)
        for k in range(top):
            hit = by_token[k : k + 1, :] == expert
            named = jnp.where(hit, 1.0, named)
            weight = jnp.where(hit, by_token[top + k : top + k + 1, :], weight)
        t_row = lax.broadcasted_iota(jnp.int32, (col, col), 0)
        t_col = lax.broadcasted_iota(jnp.int32, (col, col), 1)
        before = ((t_row < t_col) & (lax.div(t_row, tile) == lax.div(t_col, tile))).astype(BF16)
        rank = jnp.dot(named.astype(BF16), before, preferred_element_type=F32)
        return jnp.where(named > 0.5, rank, -1.0), weight

    s_row = lax.broadcasted_iota(jnp.int32, (slots, col), 0)
    s_col = lax.broadcasted_iota(jnp.int32, (slots, col), 1)
    in_block = lax.div(s_row, CAP) == lax.div(s_col, tile)
    want = jnp.where(in_block, lax.rem(s_row, CAP).astype(F32), -2.0)

    def x_index(h, g, c_):
        return (h * nx + g) * nc + c_

    def select(h, g, rank, weight):
        chosen = []
        for c_ in range(nc):
            i = g * nc + c_
            hit = rank[i : i + 1, :] == want
            chosen.append(jnp.where(hit, 1.0, 0.0).astype(BF16))
            swbuf[pl.ds(base(h, g, c_), slots), :] = jnp.where(
                hit, weight[i : i + 1, :], 0.0
            ).astype(BF16)
        xsend[pl.ds(base(h, g, 0), nc * slots), :] = jnp.dot(
            jnp.concatenate(chosen, axis=0), zbuf[h * col : (h + 1) * col, 0:quarter],
            preferred_element_type=F32,
        ).astype(BF16)
        land = ybuf.at[y, rows(base(h, g, c), slots), :]
        if g > 0:
            for c_ in range(nc):
                send(
                    xsend.at[pl.ds(base(h, g, c_), slots), :], land, x_s.at[x_index(h, g, c_)],
                    x_r.at[x_index(h, g, c)], dev(to_x(g), y, z, c_),
                )
        else:
            other = 1 - c
            send(
                xsend.at[rows(base(h, g, other), slots), :], land, x_s.at[x_index(h, g, 0)],
                x_r.at[x_index(h, g, c)], dev(x, y, z, other),
            )
            here = rows(base(h, g, c), slots)
            ybuf[y, here, :] = xsend[here, :]

    def x_wait(h, g):
        if g == 0:
            arrived(ybuf.at[y, rows(base(h, 0, 1 - c), slots), :], x_r.at[x_index(h, 0, 1 - c)])
        else:
            for c_ in range(nc):
                arrived(ybuf.at[y, pl.ds(base(h, g, c_), slots), :], x_r.at[x_index(h, g, c_)])

    y_one, y_two, p_one, p_two = {}, {}, {}, {}

    def index(h, p, n):
        return (n * 2 + h) * pairs + p

    def spread(h, p):
        x_wait(h, 2 * p)
        x_wait(h, 2 * p + 1)
        block = ybuf.at[y, pl.ds(h * each + p * pair, pair), :]
        for n, d in enumerate((1, -1)):
            i = index(h, p, n)
            y_one[h, p, d] = send(block, block, y1_s.at[i], y1_r.at[i], dev(x, at_y(d), z, c))

    def forward(h, p):
        for n, d in enumerate((1, -1)):
            y_one[h, p, d].wait_recv()
            block = ybuf.at[at_y(-d), pl.ds(h * each + p * pair + n * hp, hp), :]
            i = index(h, p, n)
            y_two[h, p, d] = send(block, block, y2_s.at[i], y2_r.at[i], dev(x, at_y(d), z, c))

    def compute(h, p):
        for d in (1, -1):
            y_two[h, p, d].wait_recv()
        here = pl.ds(h * each + p * pair, pair)
        gate = jnp.zeros((pair, wg.shape[1]), F32)
        upper = jnp.zeros((pair, wg.shape[1]), F32)
        for q in range(ny):
            piece = ybuf[q, here, :]
            deep = pl.ds(q * quarter, quarter)
            gate += jnp.dot(piece, wg[deep, :], preferred_element_type=F32)
            upper += jnp.dot(piece, wu[deep, :], preferred_element_type=F32)
        hidden = (gate / (1.0 + jnp.exp(-gate)) * upper).astype(BF16)
        for q in range(ny):
            obuf[q, here, :] = jnp.dot(
                hidden, wd[:, q * quarter : (q + 1) * quarter], preferred_element_type=F32
            ).astype(BF16)

    def give_one(h, p):
        for n, d in enumerate((1, -1)):
            i = index(h, p, n)
            p_one[h, p, d] = send(
                obuf.at[at_y(2), pl.ds(h * each + p * pair + n * hp, hp), :],
                r1buf.at[n, pl.ds((h * pairs + p) * hp, hp), :],
                p1_s.at[i], p1_r.at[i], dev(x, at_y(d), z, c),
            )

    def give_two(h, p):
        for n, d in enumerate((1, -1)):
            p_one[h, p, d].wait_recv()
            here = pl.ds(h * each + p * pair + n * hp, hp)
            q = at_y(d)
            got = r1buf[n, pl.ds((h * pairs + p) * hp, hp), :]
            obuf[q, here, :] = (obuf[q, here, :].astype(F32) + got.astype(F32)).astype(BF16)
            i = index(h, p, n)
            here = pl.ds(h * each + p * pair, pair)
            p_two[h, p, d] = send(
                obuf.at[q, here, :], r2buf.at[n, here, :],
                p2_s.at[i], p2_r.at[i], dev(x, at_y(d), z, c),
            )

    def give_back(h, p):
        for d in (1, -1):
            p_two[h, p, d].wait_recv()
        here = pl.ds(h * each + p * pair, pair)
        total = obuf[y, here, :].astype(F32) + r2buf[0, here, :].astype(F32)
        xret[here, :] = (total + r2buf[1, here, :].astype(F32)).astype(BF16)
        for g in (2 * p + 1, 2 * p):
            land = rbuf.at[rows(base(h, g, c), slots), :]
            if g > 0:
                for c_ in range(nc):
                    send(
                        xret.at[pl.ds(base(h, g, c_), slots), :], land, b_s.at[x_index(h, g, c_)],
                        b_r.at[x_index(h, g, c)], dev(from_x(g), y, z, c_),
                    )
            else:
                other = 1 - c
                send(
                    xret.at[rows(base(h, g, other), slots), :], land, b_s.at[x_index(h, g, 0)],
                    b_r.at[x_index(h, g, c)], dev(x, y, z, other),
                )
                here = rows(base(h, g, c), slots)
                rbuf[here, :] = xret[here, :]

    def combine(h, p, first):
        for g in (2 * p, 2 * p + 1):
            if g == 0:
                arrived(rbuf.at[rows(base(h, 0, 1 - c), slots), :], b_r.at[x_index(h, 0, 1 - c)])
            else:
                for c_ in range(nc):
                    arrived(rbuf.at[pl.ds(base(h, g, c_), slots), :], b_r.at[x_index(h, g, c_)])
        here = pl.ds(h * each + p * pair, pair)
        term = lax.dot_general(
            swbuf[here, :], rbuf[here, :], across, preferred_element_type=F32
        )
        dest = pl.ds(h * col, col)
        if first:
            part[dest, :] = term
        else:
            part[dest, :] += term

    reach = nz // 2
    got = {}

    def block_of(o):
        return part[pl.ds(place(o), tile), :]

    def zsend(d, k, hop, value):
        src, dst = (zs1, zr1) if hop == 1 else (zs2, zr2)
        i, n = zsem(d, k, hop), (0 if d > 0 else 1) * steps + (k - 1)
        src[n] = value.astype(BF16)
        got[d, k, hop] = (
            send(src.at[n], dst.at[n], zrs_s.at[i], zrs_r.at[i], dev(x, y, at_z(d * hop), c)), dst, n
        )

    def zget(d, k):
        total = None
        for hop in (1, 2):
            if (d, k, hop) in got:
                copy, dst, n = got[d, k, hop]
                copy.wait_recv()
                value = dst[n].astype(F32)
                total = value if total is None else total + value
        return total

    def own_hop(k):
        for d in (1, -1):
            zsend(d, k, 1, block_of(d * (reach + 1 - 2 * k)))

    def next_hop(k):
        for d in (1, -1):
            zsend(d, k + 1, 2, block_of(d * (reach - 2 * k)) + zget(d, k))

    near, far = 0, 1
    mid = steps // 2
    for d in (1, -1):
        gather_send(1, d)
    for k in range(1, mid + 1):
        gather_step(k)
    for k in range(1, mid + 1):
        for d in (1, -1):
            gather_wait(k, d, 1)
    rank, weight = routes(near)
    order = (1, 0) + tuple(range(2, nx))
    for g in order[:2]:
        select(near, g, rank, weight)
    later = list(range(mid + 1, steps + 1))
    for k in later[:-1]:
        gather_step(k)
    for g in order[2:]:
        select(near, g, rank, weight)
    spread(near, 0)
    gather_step(later[-1])
    for k in later:
        for d in (1, -1):
            gather_wait(k, d, 1)
    rank, weight = routes(far)
    for g in order:
        select(far, g, rank, weight)
    for p in range(1, pairs):
        spread(near, p)
    forward(near, 0)
    spread(far, 0)
    for p in range(1, pairs):
        forward(near, p)
    for p in range(1, pairs):
        spread(far, p)
    for load in loads:
        load.wait()
    compute(near, 0)
    forward(far, 0)
    for p in range(1, pairs):
        compute(near, p)
    for p in range(1, pairs):
        forward(far, p)
    for p in range(1, pairs):
        give_one(near, p)
    compute(far, 0)
    give_one(far, 0)
    for p in range(1, pairs):
        compute(far, p)
        give_one(far, p)
    give_one(near, 0)
    back = [(far, p) for p in range(pairs)] + [(near, p) for p in range(pairs - 1, -1, -1)]
    for h, p in back:
        give_two(h, p)
    for p in range(pairs):
        give_back(far, p)
    for p in range(pairs - 1, 0, -1):
        give_back(near, p)
    for p in range(pairs):
        combine(far, p, p == 0)
    zsend(1, 1, 2, block_of(reach))
    for k in range(1, mid + 1):
        own_hop(k)
    give_back(near, 0)
    for k in range(1, mid):
        next_hop(k)
    for p in range(pairs - 1, -1, -1):
        combine(near, p, p == pairs - 1)
    for k in range(mid + 1, steps + 1):
        own_hop(k)
    for k in range(mid, steps):
        next_hop(k)
    final = block_of(0) + zget(1, steps) + zget(-1, steps)

    count = out_ref.shape[0]
    for q in range(ny):
        fsend[q] = final[q * count : (q + 1) * count, :].astype(BF16)
    frecv[y] = fsend[y]
    tails = []
    for o in (2, 1, 3):
        tails.append(
            send(fsend.at[at_y(o)], frecv.at[y], f_s.at[o], f_r.at[o], dev(x, at_y(o), z, c))
        )
    for tail in tails:
        tail.wait_recv()
    for q in range(ny):
        out_ref[:, q * quarter : (q + 1) * quarter] = frecv[q]
    for copy in sends:
        copy.wait_send()


def on_device(tokens, expert_ids, route_logits, expert_gate, expert_up, expert_down):
    n_ep, ny = lax.axis_size("ep"), N_DP
    nx, nc = CHIPS_X, CORES
    nz = n_ep // (nx * nc)
    tile, width = tokens.shape
    hidden = expert_gate.shape[2]
    quarter = width // ny
    col, slots = nz * tile, nz * CAP
    every = nx * nc * slots
    steps = nz // 4
    dma = pltpu.SemaphoreType.DMA
    vmem = pl.BlockSpec(memory_space=pltpu.VMEM)
    hbm = pl.BlockSpec(memory_space=pl.ANY)
    flops = 6 * every * width * hidden
    units = 2 * (nx // 2) * 2
    moves = 2 * nx * nc
    return pl.pallas_call(
        functools.partial(kernel, nx, nz),
        out_shape=jax.ShapeDtypeStruct((tile // ny, width), BF16),
        in_specs=[vmem, vmem, hbm, hbm, hbm, hbm],
        out_specs=vmem,
        scratch_shapes=[
            pltpu.VMEM((width, hidden), BF16),
            pltpu.VMEM((width, hidden), BF16),
            pltpu.VMEM((hidden, width), BF16),
            pltpu.VMEM((col, quarter + 128), BF16),
            pltpu.VMEM((every, col // 2), BF16),
            pltpu.VMEM((every, quarter), BF16),
            pltpu.VMEM((ny, every, quarter), BF16),
            pltpu.VMEM((ny, every, quarter), BF16),
            pltpu.VMEM((2, every // 2, quarter), BF16),
            pltpu.VMEM((2, every, quarter), BF16),
            pltpu.VMEM((every, quarter), BF16),
            pltpu.VMEM((every, quarter), BF16),
            pltpu.VMEM((col, quarter), F32),
            pltpu.VMEM((2 * steps, tile, quarter), BF16),
            pltpu.VMEM((2 * steps, tile, quarter), BF16),
            pltpu.VMEM((2 * steps, tile, quarter), BF16),
            pltpu.VMEM((2 * steps, tile, quarter), BF16),
            pltpu.VMEM((ny, tile // ny, quarter), BF16),
            pltpu.VMEM((ny, tile // ny, quarter), BF16),
            dma((4,)),
            dma((4 * steps,)), dma((4 * steps,)),
            dma((moves,)), dma((moves,)),
            dma((units,)), dma((units,)),
            dma((units,)), dma((units,)),
            dma((units,)), dma((units,)),
            dma((units,)), dma((units,)),
            dma((moves,)), dma((moves,)),
            dma((4 * steps,)), dma((4 * steps,)),
            dma((ny,)), dma((ny,)),
        ],
        compiler_params=pltpu.CompilerParams(
            collective_id=0, has_side_effects=True, vmem_limit_bytes=56 * 1024 * 1024
        ),
        cost_estimate=pl.CostEstimate(flops=flops, bytes_accessed=8 << 20, transcendentals=0),
    )(expert_ids.T, route_logits.T, tokens, expert_gate, expert_up, expert_down)


def solution(mesh):
    placed = (
        P("ep", None),
        P("ep", None),
        P("ep", None),
        P("ep", None, "dp"),
        P("ep", None, "dp"),
        P("ep", "dp", None),
    )
    return jax.shard_map(
        on_device, mesh=mesh, in_specs=placed, out_specs=P(("ep", "dp"), None), check_vma=False
    )
```

time: 130 us -> 112 us (0.86)
  Pallas kernels: 125 us -> 110 us
  local copies, waits for them, and re-layouts: 4.07 us -> 1.37 us
    pallas_call x1, Pallas kernels: 125 us -> 110 us  [on_device(): pl.pallas_call(functools.partial(kernel, nx, nz), out_shape=jax.ShapeDtyp...]
    unnamed x3 -> x1, local copies, waits for them, and re-layouts: 4.07 us -> 1.37 us
where the time goes in v2:
time: 112 us; the launch traced here: 111 us
  Pallas kernels  110 us (98%)
  local copies, waits for them, and re-layouts  1.37 us (1%)
    pallas_call x1, Pallas kernels, on_device(): pl.pallas_call(functools.partial(kernel, nx, nz), out_shape=jax.ShapeDtyp...  110 us

profile of v2, /device:TPU:1, one launch (start us, length us, event | category | flops | bytes accessed | tf_op | source)
XLA Modules:
  0.0 111.5 jit_solution(6659560465811728675)
XLA Ops:
  0.0 110.1 %shard_map.64 = bf16[4,3584]{1,0:T(4,128)(2,1)} custom-call(s32[8,16]{1,0:T(8,128)} %bitcast.2, f32[8,16]{1,0:T(8,128)} %bitcast.3, bf16[16,3584]{1,0:T(8,128)(2,1)} %tok_hbm.1, bf16[1,3584,256]{2,1,0:T(8,128)(2,1)} %wg_hbm.1, bf16[1,3584,256]{2,1,0:T(8,128)(2,1)} %wu_hbm.1, bf16[1,256,3584]{2,1,0:T(8,128)(2,1)} %wd_hbm.1), custom_call_target="tpu_custom_call" | custom-call | flops 2818572288 | bytes 8388608 | tf_op jit(solution)/shard_map/pallas_call | solution.py:461
  110.1 1.4 %copy.8 = bf16[4,3584]{1,0:T(4,128)(2,1)} copy(bf16[4,3584]{1,0:T(4,128)(2,1)} %shard_map.64) | data formatting | bytes 57344

commit v3 on v2

--- a/solution.py
+++ b/solution.py
@@ -19,10 +19,10 @@
 
 def kernel(
     nx, nz, ids_ref, logits_ref, tok_hbm, wg_hbm, wu_hbm, wd_hbm, out_ref,
-    wg, wu, wd, zbuf, swbuf, xsend, ybuf, obuf, r1buf, r2buf, xret, rbuf, part,
-    zs1, zs2, zr1, zr2, fsend, frecv,
+    wg, wu, wd, zbuf, swbuf, xsend, ybuf, obuf, r1buf, r2buf, xret, rbuf, rbuf0, part, part0,
+    zs1, zs2, zr1, zr2, ws1, ws2, wr1, wr2, fsend, frecv,
     w_sem, zag_s, zag_r, x_s, x_r, y1_s, y1_r, y2_s, y2_r, p1_s, p1_r, p2_s, p2_r,
-    b_s, b_r, zrs_s, zrs_r, f_s, f_r,
+    b_s, b_r, zrs_s, zrs_r, wrs_s, wrs_r, f_s, f_r,
 ):
     nc, ny = CORES, N_DP
     tile, width = tok_hbm.shape
@@ -31,11 +31,10 @@
     col = nz * tile // 2
     near_blocks = nz // 2
     slots = near_blocks * CAP
-    pair = 2 * nc * slots
-    each = nx * nc * slots
-    hp = pair // 2
-    pairs = nx // 2
+    both = nc * slots
     offsets = {2: (0, 1), 4: (0, 1, 3, 2)}[nx]
+    units = {2: ((1,), (0,)), 4: ((1, 2), (3,), (0,))}[nx]
+    last = len(units) - 1
     ep = lax.axis_index("ep")
     y = lax.axis_index("dp")
     c = lax.rem(ep, nc)
@@ -66,7 +65,12 @@
         return pl.ds(pl.multiple_of(start, size), size)
 
     def base(h, g, c_):
-        return h * each + (g * nc + c_) * slots
+        if g == 0:
+            return h * both + c_ * slots
+        return 2 * both + (h * (nx - 1) + g - 1) * both + c_ * slots
+
+    def span(h, u):
+        return base(h, units[u][0], 0), len(units[u]) * both
 
     sends = []
 
@@ -84,6 +88,14 @@
             src_ref=ref, dst_ref=ref, send_sem=rsem, recv_sem=rsem,
             device_id=dev(x, y, z, 1 - c), device_id_type=MESH,
         ).wait_recv()
+
+    barrier = pltpu.get_barrier_semaphore()
+    peers = [dev(x, y, at_z(o), c) for o in (1, -1, 2, -2)]
+    peers += [dev(from_x(g), y, z, c_) for g in range(1, nx) for c_ in range(nc)]
+    peers += [dev(x, y, z, 1 - c)]
+    peers += [dev(x, at_y(o), z, c) for o in range(1, ny)]
+    for peer in peers:
+        pl.semaphore_signal(barrier, inc=1, device_id=peer, device_id_type=MESH)
 
     own = pl.ds(place(0), tile)
     mine = pltpu.make_async_copy(
@@ -102,14 +114,6 @@
         ids_ref[...].astype(F32).astype(BF16), put_id, across, preferred_element_type=F32
     ) + lax.dot_general(wts.astype(BF16), put_w, across, preferred_element_type=F32)
     zbuf[own, quarter : quarter + 128] = meta.astype(BF16)
-
-    barrier = pltpu.get_barrier_semaphore()
-    peers = [dev(x, y, at_z(o), c) for o in (1, -1, 2, -2)]
-    peers += [dev(from_x(g), y, z, c_) for g in range(1, nx) for c_ in range(nc)]
-    peers += [dev(x, y, z, 1 - c)]
-    peers += [dev(x, at_y(o), z, c) for o in range(1, ny)]
-    for peer in peers:
-        pl.semaphore_signal(barrier, inc=1, device_id=peer, device_id_type=MESH)
 
     loads = [
         pltpu.make_async_copy(s.at[0], d, w_sem.at[i])
@@ -222,30 +226,30 @@
 
     y_one, y_two, p_one, p_two = {}, {}, {}, {}
 
-    def index(h, p, n):
-        return (n * 2 + h) * pairs + p
-
-    def spread(h, p):
-        x_wait(h, 2 * p)
-        x_wait(h, 2 * p + 1)
-        block = ybuf.at[y, pl.ds(h * each + p * pair, pair), :]
+    def index(h, u, n):
+        return (n * 2 + h) * len(units) + u
+
+    def spread(h, u):
+        for g in units[u]:
+            x_wait(h, g)
+        start, size = span(h, u)
+        block = ybuf.at[y, pl.ds(start, size), :]
         for n, d in enumerate((1, -1)):
-            i = index(h, p, n)
-            y_one[h, p, d] = send(block, block, y1_s.at[i], y1_r.at[i], dev(x, at_y(d), z, c))
-
-    def forward(h, p):
+            i = index(h, u, n)
+            y_one[h, u, d] = send(block, block, y1_s.at[i], y1_r.at[i], dev(x, at_y(d), z, c))
+
+    def forward(h, u):
+        start, size = span(h, u)
         for n, d in enumerate((1, -1)):
-            y_one[h, p, d].wait_recv()
-            block = ybuf.at[at_y(-d), pl.ds(h * each + p * pair + n * hp, hp), :]
-            i = index(h, p, n)
-            y_two[h, p, d] = send(block, block, y2_s.at[i], y2_r.at[i], dev(x, at_y(d), z, c))
-
-    def compute(h, p):
-        for d in (1, -1):
-            y_two[h, p, d].wait_recv()
-        here = pl.ds(h * each + p * pair, pair)
-        gate = jnp.zeros((pair, wg.shape[1]), F32)
-        upper = jnp.zeros((pair, wg.shape[1]), F32)
+            y_one[h, u, d].wait_recv()
+            block = ybuf.at[at_y(-d), pl.ds(start + n * size // 2, size // 2), :]
+            i = index(h, u, n)
+            y_two[h, u, d] = send(block, block, y2_s.at[i], y2_r.at[i], dev(x, at_y(d), z, c))
+
+    def experts(start, size):
+        here = pl.ds(start, size)
+        gate = jnp.zeros((size, wg.shape[1]), F32)
+        upper = jnp.zeros((size, wg.shape[1]), F32)
         for q in range(ny):
             piece = ybuf[q, here, :]
             deep = pl.ds(q * quarter, quarter)
@@ -257,60 +261,84 @@
                 hidden, wd[:, q * quarter : (q + 1) * quarter], preferred_element_type=F32
             ).astype(BF16)
 
-    def give_one(h, p):
+    def compute(h, u):
+        for d in (1, -1):
+            y_two[h, u, d].wait_recv()
+        experts(*span(h, u))
+
+    home = {}
+
+    def compute_home():
+        for h in (0, 1):
+            for d in (1, -1):
+                y_two[h, last, d].wait_recv()
+        experts(0, 2 * both)
+        for h in (0, 1):
+            other = 1 - c
+            home[h] = send(
+                obuf.at[:, rows(base(h, 0, other), slots), :],
+                rbuf0.at[:, rows(base(h, 0, c), slots), :],
+                b_s.at[x_index(h, 0, 0)], b_r.at[x_index(h, 0, c)], dev(x, y, z, other),
+            )
+            here = rows(base(h, 0, c), slots)
+            for q in range(ny):
+                rbuf0[q, here, :] = obuf[q, here, :]
+
+    def combine_home():
+        for h in (0, 1):
+            arrived(
+                rbuf0.at[:, rows(base(h, 0, 1 - c), slots), :], b_r.at[x_index(h, 0, 1 - c)]
+            )
+            here = pl.ds(base(h, 0, 0), both)
+            for q in range(ny):
+                part0[h * col : (h + 1) * col, q * quarter : (q + 1) * quarter] = lax.dot_general(
+                    swbuf[here, :], rbuf0[q, here, :], across, preferred_element_type=F32
+                )
+
+    def give_one(h, u):
+        start, size = span(h, u)
         for n, d in enumerate((1, -1)):
-            i = index(h, p, n)
-            p_one[h, p, d] = send(
-                obuf.at[at_y(2), pl.ds(h * each + p * pair + n * hp, hp), :],
-                r1buf.at[n, pl.ds((h * pairs + p) * hp, hp), :],
+            i = index(h, u, n)
+            p_one[h, u, d] = send(
+                obuf.at[at_y(2), pl.ds(start + n * size // 2, size // 2), :],
+                r1buf.at[n, pl.ds(start // 2, size // 2), :],
                 p1_s.at[i], p1_r.at[i], dev(x, at_y(d), z, c),
             )
 
-    def give_two(h, p):
+    def give_two(h, u):
+        start, size = span(h, u)
         for n, d in enumerate((1, -1)):
-            p_one[h, p, d].wait_recv()
-            here = pl.ds(h * each + p * pair + n * hp, hp)
+            p_one[h, u, d].wait_recv()
+            here = pl.ds(start + n * size // 2, size // 2)
             q = at_y(d)
-            got = r1buf[n, pl.ds((h * pairs + p) * hp, hp), :]
+            got = r1buf[n, pl.ds(start // 2, size // 2), :]
             obuf[q, here, :] = (obuf[q, here, :].astype(F32) + got.astype(F32)).astype(BF16)
-            i = index(h, p, n)
-            here = pl.ds(h * each + p * pair, pair)
-            p_two[h, p, d] = send(
+            i = index(h, u, n)
+            here = pl.ds(start, size)
+            p_two[h, u, d] = send(
                 obuf.at[q, here, :], r2buf.at[n, here, :],
                 p2_s.at[i], p2_r.at[i], dev(x, at_y(d), z, c),
             )
 
-    def give_back(h, p):
+    def give_back(h, u):
         for d in (1, -1):
-            p_two[h, p, d].wait_recv()
-        here = pl.ds(h * each + p * pair, pair)
+            p_two[h, u, d].wait_recv()
+        here = pl.ds(*span(h, u))
         total = obuf[y, here, :].astype(F32) + r2buf[0, here, :].astype(F32)
         xret[here, :] = (total + r2buf[1, here, :].astype(F32)).astype(BF16)
-        for g in (2 * p + 1, 2 * p):
+        for g in units[u]:
             land = rbuf.at[rows(base(h, g, c), slots), :]
-            if g > 0:
-                for c_ in range(nc):
-                    send(
-                        xret.at[pl.ds(base(h, g, c_), slots), :], land, b_s.at[x_index(h, g, c_)],
-                        b_r.at[x_index(h, g, c)], dev(from_x(g), y, z, c_),
-                    )
-            else:
-                other = 1 - c
+            for c_ in range(nc):
                 send(
-                    xret.at[rows(base(h, g, other), slots), :], land, b_s.at[x_index(h, g, 0)],
-                    b_r.at[x_index(h, g, c)], dev(x, y, z, other),
+                    xret.at[pl.ds(base(h, g, c_), slots), :], land, b_s.at[x_index(h, g, c_)],
+                    b_r.at[x_index(h, g, c)], dev(from_x(g), y, z, c_),
                 )
-                here = rows(base(h, g, c), slots)
-                rbuf[here, :] = xret[here, :]
-
-    def combine(h, p, first):
-        for g in (2 * p, 2 * p + 1):
-            if g == 0:
-                arrived(rbuf.at[rows(base(h, 0, 1 - c), slots), :], b_r.at[x_index(h, 0, 1 - c)])
-            else:
-                for c_ in range(nc):
-                    arrived(rbuf.at[pl.ds(base(h, g, c_), slots), :], b_r.at[x_index(h, g, c_)])
-        here = pl.ds(h * each + p * pair, pair)
+
+    def combine(h, u, first):
+        for g in units[u]:
+            for c_ in range(nc):
+                arrived(rbuf.at[pl.ds(base(h, g, c_), slots), :], b_r.at[x_index(h, g, c_)])
+        here = pl.ds(*span(h, u))
         term = lax.dot_general(
             swbuf[here, :], rbuf[here, :], across, preferred_element_type=F32
         )
@@ -321,39 +349,54 @@
             part[dest, :] += term
 
     reach = nz // 2
-    got = {}
-
-    def block_of(o):
-        return part[pl.ds(place(o), tile), :]
-
-    def zsend(d, k, hop, value):
-        src, dst = (zs1, zr1) if hop == 1 else (zs2, zr2)
-        i, n = zsem(d, k, hop), (0 if d > 0 else 1) * steps + (k - 1)
-        src[n] = value.astype(BF16)
-        got[d, k, hop] = (
-            send(src.at[n], dst.at[n], zrs_s.at[i], zrs_r.at[i], dev(x, y, at_z(d * hop), c)), dst, n
-        )
-
-    def zget(d, k):
-        total = None
-        for hop in (1, 2):
-            if (d, k, hop) in got:
-                copy, dst, n = got[d, k, hop]
-                copy.wait_recv()
-                value = dst[n].astype(F32)
-                total = value if total is None else total + value
-        return total
-
-    def own_hop(k):
-        for d in (1, -1):
-            zsend(d, k, 1, block_of(d * (reach + 1 - 2 * k)))
-
-    def next_hop(k):
-        for d in (1, -1):
-            zsend(d, k + 1, 2, block_of(d * (reach - 2 * k)) + zget(d, k))
+
+    def reducer(source, src1, src2, dst1, dst2, ssem, rsem):
+        got = {}
+
+        def block_of(o):
+            return source[pl.ds(place(o), tile), :]
+
+        def zsend(d, k, hop, value):
+            src, dst = (src1, dst1) if hop == 1 else (src2, dst2)
+            i, n = zsem(d, k, hop), (0 if d > 0 else 1) * steps + (k - 1)
+            src[n] = value.astype(BF16)
+            got[d, k, hop] = (
+                send(src.at[n], dst.at[n], ssem.at[i], rsem.at[i], dev(x, y, at_z(d * hop), c)), dst, n
+            )
+
+        def zget(d, k):
+            total = None
+            for hop in (1, 2):
+                if (d, k, hop) in got:
+                    copy, dst, n = got[d, k, hop]
+                    copy.wait_recv()
+                    value = dst[n].astype(F32)
+                    total = value if total is None else total + value
+            return total
+
+        def own_hop(k):
+            if k == 1:
+                zsend(1, 1, 2, block_of(reach))
+            for d in (1, -1):
+                zsend(d, k, 1, block_of(d * (reach + 1 - 2 * k)))
+
+        def next_hop(k):
+            for d in (1, -1):
+                zsend(d, k + 1, 2, block_of(d * (reach - 2 * k)) + zget(d, k))
+
+        def finish():
+            return block_of(0) + zget(1, steps) + zget(-1, steps)
+
+        return own_hop, next_hop, finish
+
+    own_hop, next_hop, finish = reducer(part, zs1, zs2, zr1, zr2, zrs_s, zrs_r)
+    wide_own, wide_next, wide_finish = reducer(part0, ws1, ws2, wr1, wr2, wrs_s, wrs_r)
 
     near, far = 0, 1
     mid = steps // 2
+    zero = last
+    rest = tuple(range(1, last))
+    later = list(range(mid + 1, steps + 1))
     for d in (1, -1):
         gather_send(1, d)
     for k in range(1, mid + 1):
@@ -362,82 +405,105 @@
         for d in (1, -1):
             gather_wait(k, d, 1)
     rank, weight = routes(near)
-    order = (1, 0) + tuple(range(2, nx))
-    for g in order[:2]:
+    for g in range(nx):
         select(near, g, rank, weight)
-    later = list(range(mid + 1, steps + 1))
+    spread(near, zero)
     for k in later[:-1]:
         gather_step(k)
-    for g in order[2:]:
-        select(near, g, rank, weight)
     spread(near, 0)
+    forward(near, zero)
     gather_step(later[-1])
     for k in later:
         for d in (1, -1):
             gather_wait(k, d, 1)
     rank, weight = routes(far)
-    for g in order:
+    for g in range(nx):
         select(far, g, rank, weight)
-    for p in range(1, pairs):
-        spread(near, p)
+    spread(far, zero)
+    for u in rest:
+        spread(near, u)
     forward(near, 0)
     spread(far, 0)
-    for p in range(1, pairs):
-        forward(near, p)
-    for p in range(1, pairs):
-        spread(far, p)
+    forward(far, zero)
+    for u in rest:
+        forward(near, u)
+    for u in rest:
+        spread(far, u)
     for load in loads:
         load.wait()
+    compute_home()
+    forward(far, 0)
     compute(near, 0)
-    forward(far, 0)
-    for p in range(1, pairs):
-        compute(near, p)
-    for p in range(1, pairs):
-        forward(far, p)
-    for p in range(1, pairs):
-        give_one(near, p)
+    give_one(near, 0)
+    combine_home()
+    wide_own(1)
+    for u in rest:
+        forward(far, u)
+    for k in range(2, steps + 1):
+        wide_own(k)
+    for u in rest:
+        compute(near, u)
+        give_one(near, u)
+    wide_next(1)
     compute(far, 0)
     give_one(far, 0)
-    for p in range(1, pairs):
-        compute(far, p)
-        give_one(far, p)
-    give_one(near, 0)
-    back = [(far, p) for p in range(pairs)] + [(near, p) for p in range(pairs - 1, -1, -1)]
-    for h, p in back:
-        give_two(h, p)
-    for p in range(pairs):
-        give_back(far, p)
-    for p in range(pairs - 1, 0, -1):
-        give_back(near, p)
-    for p in range(pairs):
-        combine(far, p, p == 0)
-    zsend(1, 1, 2, block_of(reach))
+    for u in rest:
+        compute(far, u)
+        give_one(far, u)
+    for k in range(2, mid + 1):
+        wide_next(k)
+    give_two(far, 0)
+    for u in rest:
+        give_two(far, u)
+    for u in rest:
+        give_two(near, u)
+    give_two(near, 0)
+    for k in range(max(mid, 1) + 1, steps):
+        wide_next(k)
+    give_back(far, 0)
+    for u in rest:
+        give_back(far, u)
+    for u in rest:
+        give_back(near, u)
+    combine(far, 0, True)
+    for u in rest:
+        combine(far, u, False)
     for k in range(1, mid + 1):
         own_hop(k)
+    wide = wide_finish()
     give_back(near, 0)
     for k in range(1, mid):
         next_hop(k)
-    for p in range(pairs - 1, -1, -1):
-        combine(near, p, p == pairs - 1)
-    for k in range(mid + 1, steps + 1):
-        own_hop(k)
+    for n, u in enumerate(rest):
+        combine(near, u, n == 0)
+    combine(near, 0, not rest)
     for k in range(mid, steps):
-        next_hop(k)
-    final = block_of(0) + zget(1, steps) + zget(-1, steps)
+        if k == mid:
+            next_hop(k)
+            for j in range(mid + 1, steps + 1):
+                own_hop(j)
+        else:
+            next_hop(k)
+    main = finish()
 
     count = out_ref.shape[0]
     for q in range(ny):
-        fsend[q] = final[q * count : (q + 1) * count, :].astype(BF16)
-    frecv[y] = fsend[y]
+        piece = slice(q * quarter, (q + 1) * quarter)
+        share = (wide[:, piece] + jnp.where(y == q, main, 0.0)).astype(BF16)
+        for o in range(ny):
+            fsend[o, :, piece] = share[o * count : (o + 1) * count, :]
     tails = []
     for o in (2, 1, 3):
         tails.append(
             send(fsend.at[at_y(o)], frecv.at[y], f_s.at[o], f_r.at[o], dev(x, at_y(o), z, c))
         )
+    frecv[y] = fsend[y]
     for tail in tails:
         tail.wait_recv()
-    for q in range(ny):
-        out_ref[:, q * quarter : (q + 1) * quarter] = frecv[q]
+    total = frecv[0].astype(F32)
+    for q in range(1, ny):
+        total += frecv[q].astype(F32)
+    out_ref[...] = total.astype(BF16)
     for copy in sends:
         copy.wait_send()
 
@@ -456,7 +522,8 @@
     vmem = pl.BlockSpec(memory_space=pltpu.VMEM)
     hbm = pl.BlockSpec(memory_space=pl.ANY)
     flops = 6 * every * width * hidden
-    units = 2 * (nx // 2) * 2
+    units = 4 * (nx // 2 + 1)
+    home = 2 * nc * slots // 2
     moves = 2 * nx * nc
     return pl.pallas_call(
         functools.partial(kernel, nx, nz),
@@ -476,13 +543,19 @@
             pltpu.VMEM((2, every, quarter), BF16),
             pltpu.VMEM((every, quarter), BF16),
             pltpu.VMEM((every, quarter), BF16),
+            pltpu.VMEM((ny, home, quarter), BF16),
             pltpu.VMEM((col, quarter), F32),
+            pltpu.VMEM((col, width), F32),
             pltpu.VMEM((2 * steps, tile, quarter), BF16),
             pltpu.VMEM((2 * steps, tile, quarter), BF16),
             pltpu.VMEM((2 * steps, tile, quarter), BF16),
             pltpu.VMEM((2 * steps, tile, quarter), BF16),
-            pltpu.VMEM((ny, tile // ny, quarter), BF16),
-            pltpu.VMEM((ny, tile // ny, quarter), BF16),
+            pltpu.VMEM((2 * steps, tile, width), BF16),
+            pltpu.VMEM((2 * steps, tile, width), BF16),
+            pltpu.VMEM((2 * steps, tile, width), BF16),
+            pltpu.VMEM((2 * steps, tile, width), BF16),
+            pltpu.VMEM((ny, tile // ny, width), BF16),
+            pltpu.VMEM((ny, tile // ny, width), BF16),
             dma((4,)),
             dma((4 * steps,)), dma((4 * steps,)),
             dma((moves,)), dma((moves,)),
@@ -491,6 +564,7 @@
             dma((units,)), dma((units,)),
             dma((units,)), dma((units,)),
             dma((moves,)), dma((moves,)),
+            dma((4 * steps,)), dma((4 * steps,)),
             dma((4 * steps,)), dma((4 * steps,)),
             dma((ny,)), dma((ny,)),
         ],

time: 112 us -> 117 us (1.045); the launches traced: 111 us -> 115 us
  Pallas kernels: 110 us -> 113 us
    pallas_call x1, Pallas kernels: 110 us -> 113 us  [on_device(): pl.pallas_call(functools.partial(kernel, nx, nz), out_shape=jax.ShapeDtyp...]
where the time goes in v3:
time: 117 us; the launch traced here: 115 us
  Pallas kernels  113 us (97%)
  local copies, waits for them, and re-layouts  1.37 us (1%)
    pallas_call x1, Pallas kernels, on_device(): pl.pallas_call(functools.partial(kernel, nx, nz), out_shape=jax.ShapeDtyp...  113 us

profile of v3, /device:TPU:1, one launch (start us, length us, event | category | flops | bytes accessed | tf_op | source)
XLA Modules:
  0.0 114.9 jit_solution(2753207408191166132)
XLA Ops:
  0.0 113.5 %shard_map.64 = bf16[4,3584]{1,0:T(4,128)(2,1)} custom-call(s32[8,16]{1,0:T(8,128)} %bitcast.2, f32[8,16]{1,0:T(8,128)} %bitcast.3, bf16[16,3584]{1,0:T(8,128)(2,1)} %tok_hbm.1, bf16[1,3584,256]{2,1,0:T(8,128)(2,1)} %wg_hbm.1, bf16[1,3584,256]{2,1,0:T(8,128)(2,1)} %wu_hbm.1, bf16[1,256,3584]{2,1,0:T(8,128)(2,1)} %wd_hbm.1), custom_call_target="tpu_custom_call" | custom-call | flops 2818572288 | bytes 8388608 | tf_op jit(solution)/shard_map/pallas_call | solution.py:528
  113.5 1.4 %copy.8 = bf16[4,3584]{1,0:T(4,128)(2,1)} copy(bf16[4,3584]{1,0:T(4,128)(2,1)} %shard_map.64) | data formatting | bytes 57344

commit v4 on v3

v4 whole, which is shorter than its diff:
```python
import functools

import jax
import jax.numpy as jnp
from jax import lax
from jax.experimental import pallas as pl
from jax.experimental.pallas import tpu as pltpu
from jax.sharding import PartitionSpec as P

MESH = pl.DeviceIdType.MESH
F32 = jnp.float32
BF16 = jnp.bfloat16
ROUTE_SCALE = 2.5
CAP = 4
CHIPS_X = 4
CORES = 2
N_DP = 4


def kernel(
    nx, nz, ids_ref, logits_ref, tok_hbm, wg_hbm, wu_hbm, wd_hbm, out_ref,
    wg, wu, wd, zbuf, swbuf, xsend, ybuf, obuf, r1buf, r2buf, xret, rbuf, rbuf0, part, part0,
    zs, zr, ws, wr, fsend, frecv,
    w_sem, s_sem, zag_r, zag_one, x_r, y1_r, y2_r, p1_r, p2_r, b_r, zrs_r, wrs_r, f_r,
):
    nc, ny = CORES, N_DP
    tile, width = tok_hbm.shape
    quarter = width // ny
    top = ids_ref.shape[0]
    col = nz * tile // 2
    near_blocks = nz // 2
    slots = near_blocks * CAP
    both = nc * slots
    offsets = {2: (0, 1), 4: (0, 1, 3, 2)}[nx]
    units = {2: ((1,), (0,)), 4: ((1, 2), (3,), (0,))}[nx]
    last = len(units) - 1
    (zag_s, x_s, y1_s, y2_s, p1_s, p2_s, b_s, home_s, zrs_s, wrs_s, f_s) = [
        s_sem.at[i] for i in range(11)
    ]
    ep = lax.axis_index("ep")
    y = lax.axis_index("dp")
    c = lax.rem(ep, nc)
    z = lax.rem(lax.div(ep, nc), nz)
    x = lax.div(ep, nc * nz)

    def dev(x_, y_, z_, c_):
        return (((x_ * nz + z_) * nc + c_), y_)

    def to_x(g):
        return lax.rem(x + (nx - offsets[g]), nx)

    def from_x(g):
        return lax.rem(x + offsets[g], nx)

    def at_y(o):
        return lax.rem(y + (o + ny), ny)

    def at_z(o):
        return lax.rem(z + (o + nz), nz)

    def place(o):
        return ((o + nz // 4) % nz) * tile

    def rows(start, size):
        if isinstance(start, int):
            return pl.ds(start, size)
        return pl.ds(pl.multiple_of(start, size), size)

    def base(h, g, c_):
        if g == 0:
            return h * both + c_ * slots
        return 2 * both + (h * (nx - 1) + g - 1) * both + c_ * slots

    def span(h, u):
        return base(h, units[u][0], 0), len(units[u]) * both

    def send(src, dst, ssem, rsem, device):
        pltpu.make_async_remote_copy(
            src_ref=src, dst_ref=dst, send_sem=ssem, recv_sem=rsem,
            device_id=device, device_id_type=MESH,
        ).start()

    def awaits(ref, sem):
        return pltpu.make_async_remote_copy(
            src_ref=ref, dst_ref=ref, send_sem=sem, recv_sem=sem,
            device_id=dev(x, y, z, 1 - c), device_id_type=MESH,
        )

    def arrived(ref, sem):
        awaits(ref, sem).wait_recv()

    barrier = pltpu.get_barrier_semaphore()
    peers = [dev(x, y, at_z(o), c) for o in (1, -1, 2, -2)]
    peers += [dev(from_x(g), y, z, c_) for g in range(1, nx) for c_ in range(nc)]
    peers += [dev(x, y, z, 1 - c)]
    peers += [dev(x, at_y(o), z, c) for o in range(1, ny)]
    for peer in peers:
        pl.semaphore_signal(barrier, inc=1, device_id=peer, device_id_type=MESH)

    own = pl.ds(place(0), tile)
    mine = pltpu.make_async_copy(
        tok_hbm.at[:, pl.ds(pl.multiple_of(y * quarter, 128), quarter)],
        zbuf.at[own, pl.ds(0, quarter)], w_sem.at[3],
    )
    mine.start()
    scores = 1.0 / (1.0 + jnp.exp(-logits_ref[...]))
    wts = ROUTE_SCALE * scores / jnp.sum(scores, axis=0, keepdims=True)
    lane = lax.broadcasted_iota(jnp.int32, (top, 128), 1)
    sub = lax.broadcasted_iota(jnp.int32, (top, 128), 0)
    put_id = (lane == sub).astype(BF16)
    put_w = (lane == sub + top).astype(BF16)
    across = (((0,), (0,)), ((), ()))
    meta = lax.dot_general(
        ids_ref[...].astype(F32).astype(BF16), put_id, across, preferred_element_type=F32
    ) + lax.dot_general(wts.astype(BF16), put_w, across, preferred_element_type=F32)
    zbuf[own, quarter : quarter + 128] = meta.astype(BF16)

    loads = [
        pltpu.make_async_copy(s.at[0], d, w_sem.at[i])
        for i, (s, d) in enumerate(((wg_hbm, wg), (wu_hbm, wu), (wd_hbm, wd)))
    ]
    for load in loads:
        load.start()
    mine.wait()
    pl.semaphore_wait(barrier, len(peers))

    steps = nz // 4

    def zslot(d, k):
        return (0 if d > 0 else 1) * steps + (k - 1)

    mid = steps // 2

    def gather_send(k, d):
        o = -d * 2 * (k - 1)
        for hop in (2, 1):
            if hop == 2 and d < 0 and k == steps:
                continue
            rsem = zag_r.at[zslot(d, k)] if hop == 2 else zag_one.at[0 if k <= mid else 1]
            send(
                zbuf.at[pl.ds(place(o), tile), :], zbuf.at[pl.ds(place(o - d * hop), tile), :],
                zag_s, rsem, dev(x, y, at_z(d * hop), c),
            )

    def gather_step(k):
        for d in (1, -1):
            if d > 0 or k < steps:
                arrived(zbuf.at[pl.ds(0, tile), :], zag_r.at[zslot(d, k)])
            if k < steps:
                gather_send(k + 1, d)

    def gather_rest(h):
        count = mid if h == 0 else steps - mid
        arrived(zbuf.at[pl.ds(0, 2 * count * tile), :], zag_one.at[h])

    def routes(h):
        pick = (
            lax.broadcasted_iota(jnp.int32, (2 * top, 128), 0)
            == lax.broadcasted_iota(jnp.int32, (2 * top, 128), 1)
        ).astype(BF16)
        by_token = lax.dot_general(
            pick, zbuf[h * col : (h + 1) * col, quarter : quarter + 128],
            (((1,), (1,)), ((), ())), preferred_element_type=F32,
        )
        lanes = nx * nc
        j = lax.broadcasted_iota(jnp.int32, (lanes, col), 0)
        jg, jc = lax.div(j, nc), lax.rem(j, nc)
        off = jnp.zeros_like(jg)
        for g, o in enumerate(offsets):
            off = jnp.where(jg == g, nx - o, off)
        expert = ((lax.rem(x + off, nx) * nz + z) * nc + jc).astype(F32)
        named = jnp.zeros((lanes, col), F32)
        weight = jnp.zeros((lanes, col), F32)
        for k in range(top):
            hit = by_token[k : k + 1, :] == expert
            named = jnp.where(hit, 1.0, named)
            weight = jnp.where(hit, by_token[top + k : top + k + 1, :], weight)
        t_row = lax.broadcasted_iota(jnp.int32, (col, col), 0)
        t_col = lax.broadcasted_iota(jnp.int32, (col, col), 1)
        before = ((t_row < t_col) & (lax.div(t_row, tile) == lax.div(t_col, tile))).astype(BF16)
        rank = jnp.dot(named.astype(BF16), before, preferred_element_type=F32)
        return jnp.where(named > 0.5, rank, -1.0), weight

    s_row = lax.broadcasted_iota(jnp.int32, (slots, col), 0)
    s_col = lax.broadcasted_iota(jnp.int32, (slots, col), 1)
    in_block = lax.div(s_row, CAP) == lax.div(s_col, tile)
    want = jnp.where(in_block, lax.rem(s_row, CAP).astype(F32), -2.0)

    unit_of = {g: u for u, unit in enumerate(units) for g in unit}

    def x_index(h, g):
        return h * len(units) + unit_of[g]

    def select(h, g, rank, weight):
        chosen = []
        for c_ in range(nc):
            i = g * nc + c_
            hit = rank[i : i + 1, :] == want
            chosen.append(jnp.where(hit, 1.0, 0.0).astype(BF16))
            swbuf[pl.ds(base(h, g, c_), slots), :] = jnp.where(
                hit, weight[i : i + 1, :], 0.0
            ).astype(BF16)
        xsend[pl.ds(base(h, g, 0), nc * slots), :] = jnp.dot(
            jnp.concatenate(chosen, axis=0), zbuf[h * col : (h + 1) * col, 0:quarter],
            preferred_element_type=F32,
        ).astype(BF16)
        land = ybuf.at[y, rows(base(h, g, c), slots), :]
        if g > 0:
            for c_ in range(nc):
                send(
                    xsend.at[pl.ds(base(h, g, c_), slots), :], land, x_s,
                    x_r.at[x_index(h, g)], dev(to_x(g), y, z, c_),
                )
        else:
            other = 1 - c
            send(
                xsend.at[rows(base(h, g, other), slots), :], land, x_s,
                x_r.at[x_index(h, g)], dev(x, y, z, other),
            )
            here = rows(base(h, g, c), slots)
            ybuf[y, here, :] = xsend[here, :]

    def x_wait(h, u):
        start, size = span(h, u)
        size = slots if u == last else size
        arrived(ybuf.at[y, pl.ds(start, size), :], x_r.at[h * len(units) + u])

    def index(h, u):
        return h * len(units) + u

    def spread(h, u):
        x_wait(h, u)
        start, size = span(h, u)
        block = ybuf.at[y, pl.ds(start, size), :]
        for d in (1, -1):
            send(block, block, y1_s, y1_r.at[index(h, u)], dev(x, at_y(d), z, c))

    def forward(h, u):
        start, size = span(h, u)
        arrived(ybuf.at[pl.ds(0, 2), pl.ds(start, size), :], y1_r.at[index(h, u)])
        for n, d in enumerate((1, -1)):
            block = ybuf.at[at_y(-d), pl.ds(start + n * size // 2, size // 2), :]
            send(block, block, y2_s, y2_r.at[index(h, u)], dev(x, at_y(d), z, c))

    def y_wait(h, u):
        arrived(ybuf.at[0, pl.ds(*span(h, u)), :], y2_r.at[index(h, u)])

    def experts(start, size):
        here = pl.ds(start, size)
        gate = jnp.zeros((size, wg.shape[1]), F32)
        upper = jnp.zeros((size, wg.shape[1]), F32)
        for q in range(ny):
            piece = ybuf[q, here, :]
            deep = pl.ds(q * quarter, quarter)
            gate += jnp.dot(piece, wg[deep, :], preferred_element_type=F32)
            upper += jnp.dot(piece, wu[deep, :], preferred_element_type=F32)
        hidden = (gate / (1.0 + jnp.exp(-gate)) * upper).astype(BF16)
        for q in range(ny):
            obuf[q, here, :] = jnp.dot(
                hidden, wd[:, q * quarter : (q + 1) * quarter], preferred_element_type=F32
            ).astype(BF16)

    def compute(h, u):
        y_wait(h, u)
        experts(*span(h, u))

    def compute_home():
        for h in (0, 1):
            y_wait(h, last)
        experts(0, 2 * both)
        for h in (0, 1):
            other = 1 - c
            send(
                obuf.at[:, rows(base(h, 0, other), slots), :],
                rbuf0.at[:, rows(base(h, 0, c), slots), :],
                home_s, b_r.at[index(h, last)], dev(x, y, z, other),
            )
            here = rows(base(h, 0, c), slots)
            for q in range(ny):
                rbuf0[q, here, :] = obuf[q, here, :]

    def combine_home():
        for h in (0, 1):
            arrived(rbuf0.at[:, pl.ds(base(h, 0, 0), slots), :], b_r.at[index(h, last)])
            here = pl.ds(base(h, 0, 0), both)
            for o in range(ny):
                term = lax.dot_general(
                    swbuf[here, :], rbuf0[at_y(o), here, :], across, preferred_element_type=F32
                )
                if o == 0:
                    part[h * col : (h + 1) * col, :] = term
                else:
                    part0[h * col : (h + 1) * col, (o - 1) * quarter : o * quarter] = term

    def give_one(h, u):
        start, size = span(h, u)
        for n, d in enumerate((1, -1)):
            send(
                obuf.at[at_y(2), pl.ds(start + n * size // 2, size // 2), :],
                r1buf.at[n, pl.ds(start // 2, size // 2), :],
                p1_s, p1_r.at[index(h, u)], dev(x, at_y(d), z, c),
            )

    def give_two(h, u):
        start, size = span(h, u)
        arrived(r1buf.at[:, pl.ds(start // 2, size // 2), :], p1_r.at[index(h, u)])
        for n, d in enumerate((1, -1)):
            here = pl.ds(start + n * size // 2, size // 2)
            q = at_y(d)
            got = r1buf[n, pl.ds(start // 2, size // 2), :]
            obuf[q, here, :] = (obuf[q, here, :].astype(F32) + got.astype(F32)).astype(BF16)
            here = pl.ds(start, size)
            send(
                obuf.at[q, here, :], r2buf.at[n, here, :],
                p2_s, p2_r.at[index(h, u)], dev(x, at_y(d), z, c),
            )

    def give_back(h, u):
        here = pl.ds(*span(h, u))
        arrived(r2buf.at[:, here, :], p2_r.at[index(h, u)])
        total = obuf[y, here, :].astype(F32) + r2buf[0, here, :].astype(F32)
        xret[here, :] = (total + r2buf[1, here, :].astype(F32)).astype(BF16)
        for g in units[u]:
            land = rbuf.at[rows(base(h, g, c), slots), :]
            for c_ in range(nc):
                send(
                    xret.at[pl.ds(base(h, g, c_), slots), :], land, b_s,
                    b_r.at[index(h, u)], dev(from_x(g), y, z, c_),
                )

    def combine(h, u):
        here = pl.ds(*span(h, u))
        arrived(rbuf.at[here, :], b_r.at[index(h, u)])
        part[h * col : (h + 1) * col, :] += lax.dot_general(
            swbuf[here, :], rbuf[here, :], across, preferred_element_type=F32
        )

    reach = nz // 2

    def reducer(source, src, dst, ssem, rsem):
        def block_of(o):
            return source[pl.ds(place(o), tile), :]

        def zsend(d, k, hop, value):
            n = zslot(d, k)
            src[n, hop - 1] = value.astype(BF16)
            send(src.at[n, hop - 1], dst.at[n, hop - 1], ssem, rsem.at[n], dev(x, y, at_z(d * hop), c))

        def zget(d, k):
            n = zslot(d, k)
            if d < 0 and k == 1:
                arrived(dst.at[n, 0], rsem.at[n])
                return dst[n, 0].astype(F32)
            arrived(dst.at[n], rsem.at[n])
            return dst[n, 0].astype(F32) + dst[n, 1].astype(F32)

        def own_hop(k):
            if k == 1:
                zsend(1, 1, 2, block_of(reach))
            for d in (1, -1):
                zsend(d, k, 1, block_of(d * (reach + 1 - 2 * k)))

        def next_hop(k):
            for d in (1, -1):
                zsend(d, k + 1, 2, block_of(d * (reach - 2 * k)) + zget(d, k))

        def finish():
            return block_of(0) + zget(1, steps) + zget(-1, steps)

        return own_hop, next_hop, finish

    own_hop, next_hop, finish = reducer(part, zs, zr, zrs_s, zrs_r)
    wide_own, wide_next, wide_finish = reducer(part0, ws, wr, wrs_s, wrs_r)

    near, far = 0, 1
    rest = tuple(range(1, last))

    def wide_step(k):
        if k < steps:
            wide_next(k)
            wide_own(k + 1)

    for d in (1, -1):
        gather_send(1, d)
    for k in range(1, mid + 1):
        gather_step(k)
    gather_rest(near)
    rank, weight = routes(near)
    for g in range(nx):
        select(near, g, rank, weight)
    spread(near, last)
    for k in range(mid + 1, steps):
        gather_step(k)
    spread(near, 0)
    forward(near, last)
    gather_step(steps)
    gather_rest(far)
    rank, weight = routes(far)
    for g in range(nx):
        select(far, g, rank, weight)
    spread(far, last)
    for u in rest:
        spread(near, u)
    forward(near, 0)
    forward(far, last)
    spread(far, 0)
    for u in rest:
        forward(near, u)
        spread(far, u)
    for load in loads:
        load.wait()
    compute_home()
    compute(near, 0)
    give_one(near, 0)
    combine_home()
    wide_own(1)
    forward(far, 0)
    for u in rest:
        compute(near, u)
        give_one(near, u)
        forward(far, u)
    wide_step(1)
    for u in rest:
        give_two(near, u)
    compute(far, 0)
    give_one(far, 0)
    for u in rest:
        compute(far, u)
        give_one(far, u)
    wide_step(2)
    give_two(far, 0)
    for u in rest:
        give_two(far, u)
    give_two(near, 0)
    for k in range(3, steps):
        wide_step(k)
    for u in rest:
        give_back(near, u)
    give_back(far, 0)
    for u in rest:
        give_back(far, u)
    for u in range(last):
        combine(far, u)
    for k in range(1, mid + 1):
        own_hop(k)
    wide = wide_finish()
    for k in range(1, mid):
        next_hop(k)
    give_back(near, 0)
    for u in rest:
        combine(near, u)
    combine(near, 0)
    next_hop(mid)
    for k in range(mid + 1, steps + 1):
        own_hop(k)
    for k in range(mid + 1, steps):
        next_hop(k)
    main = finish()

    count = out_ref.shape[0]
    for o in range(ny):
        share = (main if o == 0 else wide[:, (o - 1) * quarter : o * quarter]).astype(BF16)
        piece = pl.ds(pl.multiple_of(at_y(o) * quarter, 128), quarter)
        for n in range(ny):
            fsend[n, :, piece] = share[n * count : (n + 1) * count, :]
    for o in (2, 1, 3):
        send(fsend.at[at_y(o)], frecv.at[y], f_s, f_r.at[0], dev(x, at_y(o), z, c))
    frecv[y] = fsend[y]
    arrived(frecv.at[pl.ds(0, ny - 1)], f_r.at[0])
    total = frecv[0].astype(F32)
    for q in range(1, ny):
        total += frecv[q].astype(F32)
    out_ref[...] = total.astype(BF16)

    every = ybuf.shape[1]
    moved = every - 2 * both
    for sem, ref in (
        (zag_s, zbuf.at[pl.ds(0, (nz - 1) * tile), :]),
        (x_s, xsend.at[pl.ds(0, 2 * (nx * nc - 1) * slots), :]),
        (y1_s, ybuf.at[pl.ds(0, 2), :, :]),
        (y2_s, ybuf.at[0]),
        (p1_s, ybuf.at[0, pl.ds(0, moved), :]),
        (p2_s, r2buf.at[:, pl.ds(0, moved), :]),
        (b_s, xret.at[pl.ds(0, moved), :]),
        (home_s, rbuf0.at[:, pl.ds(0, 2 * slots), :]),
        (zrs_s, ybuf.at[0, pl.ds(0, (nz - 1) * tile), :]),
        (wrs_s, part0.at[pl.ds(0, (nz - 1) * tile // 2), :]),
        (f_s, fsend.at[pl.ds(0, ny - 1)]),
    ):
        awaits(ref, sem).wait_send()


def on_device(tokens, expert_ids, route_logits, expert_gate, expert_up, expert_down):
    n_ep, ny = lax.axis_size("ep"), N_DP
    nx, nc = CHIPS_X, CORES
    nz = n_ep // (nx * nc)
    tile, width = tokens.shape
    hidden = expert_gate.shape[2]
    quarter = width // ny
    col, slots = nz * tile, nz * CAP
    every = nx * nc * slots
    steps = nz // 4
    dma = pltpu.SemaphoreType.DMA
    vmem = pl.BlockSpec(memory_space=pltpu.VMEM)
    hbm = pl.BlockSpec(memory_space=pl.ANY)
    flops = 6 * every * width * hidden
    units = 2 * (nx // 2 + 1)
    home = 2 * nc * slots // 2
    return pl.pallas_call(
        functools.partial(kernel, nx, nz),
        out_shape=jax.ShapeDtypeStruct((tile // ny, width), BF16),
        in_specs=[vmem, vmem, hbm, hbm, hbm, hbm],
        out_specs=vmem,
        scratch_shapes=[
            pltpu.VMEM((width, hidden), BF16),
            pltpu.VMEM((width, hidden), BF16),
            pltpu.VMEM((hidden, width), BF16),
            pltpu.VMEM((col, quarter + 128), BF16),
            pltpu.VMEM((every, col // 2), BF16),
            pltpu.VMEM((every, quarter), BF16),
            pltpu.VMEM((ny, every, quarter), BF16),
            pltpu.VMEM((ny, every, quarter), BF16),
            pltpu.VMEM((2, every // 2, quarter), BF16),
            pltpu.VMEM((2, every, quarter), BF16),
            pltpu.VMEM((every, quarter), BF16),
            pltpu.VMEM((every, quarter), BF16),
            pltpu.VMEM((ny, home, quarter), BF16),
            pltpu.VMEM((col, quarter), F32),
            pltpu.VMEM((col, width - quarter), F32),
            pltpu.VMEM((2 * steps, 2, tile, quarter), BF16),
            pltpu.VMEM((2 * steps, 2, tile, quarter), BF16),
            pltpu.VMEM((2 * steps, 2, tile, width - quarter), BF16),
            pltpu.VMEM((2 * steps, 2, tile, width - quarter), BF16),
            pltpu.VMEM((ny, tile // ny, width), BF16),
            pltpu.VMEM((ny, tile // ny, width), BF16),
            dma((4,)),
            dma((11,)),
            dma((2 * steps,)), dma((2,)),
            dma((units,)), dma((units,)), dma((units,)), dma((units,)), dma((units,)), dma((units,)),
            dma((2 * steps,)), dma((2 * steps,)), dma((1,)),
        ],
        compiler_params=pltpu.CompilerParams(
            collective_id=0, has_side_effects=True, vmem_limit_bytes=56 * 1024 * 1024
        ),
        cost_estimate=pl.CostEstimate(flops=flops, bytes_accessed=8 << 20, transcendentals=0),
    )(expert_ids.T, route_logits.T, tokens, expert_gate, expert_up, expert_down)


def solution(mesh):
    placed = (
        P("ep", None),
        P("ep", None),
        P("ep", None),
        P("ep", None, "dp"),
        P("ep", None, "dp"),
        P("ep", "dp", None),
    )
    return jax.shard_map(
        on_device, mesh=mesh, in_specs=placed, out_specs=P(("ep", "dp"), None), check_vma=False
    )
```

time: 117 us -> 106 us (0.906); the launches traced: 115 us -> 105 us
  Pallas kernels: 113 us -> 104 us
    pallas_call x1, Pallas kernels: 113 us -> 104 us  [on_device(): pl.pallas_call(functools.partial(kernel, nx, nz), out_shape=jax.ShapeDtyp...]
where the time goes in v4:
time: 106 us; the launch traced here: 105 us
  Pallas kernels  104 us (98%)
  local copies, waits for them, and re-layouts  1.37 us (1%)
    pallas_call x1, Pallas kernels, on_device(): pl.pallas_call(functools.partial(kernel, nx, nz), out_shape=jax.ShapeDtyp...  104 us

profile of v4, /device:TPU:1, one launch (start us, length us, event | category | flops | bytes accessed | tf_op | source)
XLA Modules:
  0.0 105.4 jit_solution(15253328538879884318)
XLA Ops:
  0.0 104.1 %shard_map.64 = bf16[4,3584]{1,0:T(4,128)(2,1)} custom-call(s32[8,16]{1,0:T(8,128)} %bitcast.2, f32[8,16]{1,0:T(8,128)} %bitcast.3, bf16[16,3584]{1,0:T(8,128)(2,1)} %tok_hbm.1, bf16[1,3584,256]{2,1,0:T(8,128)(2,1)} %wg_hbm.1, bf16[1,3584,256]{2,1,0:T(8,128)(2,1)} %wu_hbm.1, bf16[1,256,3584]{2,1,0:T(8,128)(2,1)} %wd_hbm.1), custom_call_target="tpu_custom_call" | custom-call | flops 2818572288 | bytes 8388608 | tf_op jit(solution)/shard_map/pallas_call | solution.py:509
  104.1 1.4 %copy.8 = bf16[4,3584]{1,0:T(4,128)(2,1)} copy(bf16[4,3584]{1,0:T(4,128)(2,1)} %shard_map.64) | data formatting | bytes 57344

commit v5 on v4

--- a/solution.py
+++ b/solution.py
@@ -27,13 +27,27 @@
     tile, width = tok_hbm.shape
     quarter = width // ny
     top = ids_ref.shape[0]
-    col = nz * tile // 2
-    near_blocks = nz // 2
-    slots = near_blocks * CAP
-    both = nc * slots
+    steps = nz // 4
+    mid = steps // 2
+    parts = [(-2, -1, 0, 1)]
+    if nz > 8:
+        parts.append((2, 3, -4, -3))
+    parts.append(tuple(range(nz // 4 if nz > 8 else 2, nz - (4 if nz > 8 else 2))))
+    far = len(parts) - 1
+    order = [o % nz for part_ in parts for o in part_]
+    starts = [sum(len(p) for p in parts[:i]) for i in range(len(parts))]
+    slots = [len(p) * CAP for p in parts]
+    both = [nc * n for n in slots]
+    home_rows = sum(both)
     offsets = {2: (0, 1), 4: (0, 1, 3, 2)}[nx]
-    units = {2: ((1,), (0,)), 4: ((1, 2), (3,), (0,))}[nx]
-    last = len(units) - 1
+    units = [
+        {2: ((1,), (0,)), 4: ((1, 2, 3), (0,)) if h < far else ((3,), (1, 2), (0,))}[nx]
+        for h in range(len(parts))
+    ]
+    unit_index = {}
+    for h in range(len(parts)):
+        for u in range(len(units[h])):
+            unit_index[h, u] = len(unit_index)
     (zag_s, x_s, y1_s, y2_s, p1_s, p2_s, b_s, home_s, zrs_s, wrs_s, f_s) = [
         s_sem.at[i] for i in range(11)
     ]
@@ -59,7 +73,10 @@
         return lax.rem(z + (o + nz), nz)
 
     def place(o):
-        return ((o + nz // 4) % nz) * tile
+        return order.index(o % nz) * tile
+
+    def tokens_of(h):
+        return starts[h] * tile, len(parts[h]) * tile
 
     def rows(start, size):
         if isinstance(start, int):
@@ -68,11 +85,19 @@
 
     def base(h, g, c_):
         if g == 0:
-            return h * both + c_ * slots
-        return 2 * both + (h * (nx - 1) + g - 1) * both + c_ * slots
+            return sum(both[:h]) + c_ * slots[h]
+        done = sum(both[:h]) * (nx - 1)
+        return home_rows + done + (g - 1) * both[h] + c_ * slots[h]
 
     def span(h, u):
-        return base(h, units[u][0], 0), len(units[u]) * both
+        first = min(units[h][u])
+        return base(h, first, 0), len(units[h][u]) * both[h]
+
+    def index(h, u):
+        return unit_index[h, u]
+
+    def home(h):
+        return len(units[h]) - 1
 
     def send(src, dst, ssem, rsem, device):
         pltpu.make_async_remote_copy(
@@ -124,19 +149,18 @@
     mine.wait()
     pl.semaphore_wait(barrier, len(peers))
 
-    steps = nz // 4
-
     def zslot(d, k):
         return (0 if d > 0 else 1) * steps + (k - 1)
 
-    mid = steps // 2
+    def ready(k):
+        return min(k - 1, far)
 
     def gather_send(k, d):
         o = -d * 2 * (k - 1)
         for hop in (2, 1):
             if hop == 2 and d < 0 and k == steps:
                 continue
-            rsem = zag_r.at[zslot(d, k)] if hop == 2 else zag_one.at[0 if k <= mid else 1]
+            rsem = zag_r.at[zslot(d, k)] if hop == 2 else zag_one.at[ready(k)]
             send(
                 zbuf.at[pl.ds(place(o), tile), :], zbuf.at[pl.ds(place(o - d * hop), tile), :],
                 zag_s, rsem, dev(x, y, at_z(d * hop), c),
@@ -150,16 +174,17 @@
                 gather_send(k + 1, d)
 
     def gather_rest(h):
-        count = mid if h == 0 else steps - mid
+        count = sum(ready(k) == h for k in range(1, steps + 1))
         arrived(zbuf.at[pl.ds(0, 2 * count * tile), :], zag_one.at[h])
 
     def routes(h):
+        first, col = tokens_of(h)
         pick = (
             lax.broadcasted_iota(jnp.int32, (2 * top, 128), 0)
             == lax.broadcasted_iota(jnp.int32, (2 * top, 128), 1)
         ).astype(BF16)
         by_token = lax.dot_general(
-            pick, zbuf[h * col : (h + 1) * col, quarter : quarter + 128],
+            pick, zbuf[first : first + col, quarter : quarter + 128],
             (((1,), (1,)), ((), ())), preferred_element_type=F32,
         )
         lanes = nx * nc
@@ -181,52 +206,48 @@
         rank = jnp.dot(named.astype(BF16), before, preferred_element_type=F32)
         return jnp.where(named > 0.5, rank, -1.0), weight
 
-    s_row = lax.broadcasted_iota(jnp.int32, (slots, col), 0)
-    s_col = lax.broadcasted_iota(jnp.int32, (slots, col), 1)
-    in_block = lax.div(s_row, CAP) == lax.div(s_col, tile)
-    want = jnp.where(in_block, lax.rem(s_row, CAP).astype(F32), -2.0)
-
-    unit_of = {g: u for u, unit in enumerate(units) for g in unit}
-
-    def x_index(h, g):
-        return h * len(units) + unit_of[g]
+    def unit_of(h, g):
+        return [g in unit for unit in units[h]].index(True)
 
     def select(h, g, rank, weight):
+        first, col = tokens_of(h)
+        s_row = lax.broadcasted_iota(jnp.int32, (slots[h], col), 0)
+        s_col = lax.broadcasted_iota(jnp.int32, (slots[h], col), 1)
+        in_block = lax.div(s_row, CAP) == lax.div(s_col, tile)
+        want = jnp.where(in_block, lax.rem(s_row, CAP).astype(F32), -2.0)
+        recv = x_r.at[index(h, unit_of(h, g))]
         chosen = []
         for c_ in range(nc):
             i = g * nc + c_
             hit = rank[i : i + 1, :] == want
             chosen.append(jnp.where(hit, 1.0, 0.0).astype(BF16))
-            swbuf[pl.ds(base(h, g, c_), slots), :] = jnp.where(
+            swbuf[pl.ds(base(h, g, c_), slots[h]), 0:col] = jnp.where(
                 hit, weight[i : i + 1, :], 0.0
             ).astype(BF16)
-        xsend[pl.ds(base(h, g, 0), nc * slots), :] = jnp.dot(
-            jnp.concatenate(chosen, axis=0), zbuf[h * col : (h + 1) * col, 0:quarter],
+        xsend[pl.ds(base(h, g, 0), both[h]), :] = jnp.dot(
+            jnp.concatenate(chosen, axis=0), zbuf[first : first + col, 0:quarter],
             preferred_element_type=F32,
         ).astype(BF16)
-        land = ybuf.at[y, rows(base(h, g, c), slots), :]
+        land = ybuf.at[y, rows(base(h, g, c), slots[h]), :]
         if g > 0:
             for c_ in range(nc):
                 send(
-                    xsend.at[pl.ds(base(h, g, c_), slots), :], land, x_s,
-                    x_r.at[x_index(h, g)], dev(to_x(g), y, z, c_),
+                    xsend.at[pl.ds(base(h, g, c_), slots[h]), :], land, x_s,
+                    recv, dev(to_x(g), y, z, c_),
                 )
         else:
             other = 1 - c
             send(
-                xsend.at[rows(base(h, g, other), slots), :], land, x_s,
-                x_r.at[x_index(h, g)], dev(x, y, z, other),
+                xsend.at[rows(base(h, g, other), slots[h]), :], land, x_s,
+                recv, dev(x, y, z, other),
             )
-            here = rows(base(h, g, c), slots)
+            here = rows(base(h, g, c), slots[h])
             ybuf[y, here, :] = xsend[here, :]
 
     def x_wait(h, u):
         start, size = span(h, u)
-        size = slots if u == last else size
-        arrived(ybuf.at[y, pl.ds(start, size), :], x_r.at[h * len(units) + u])
-
-    def index(h, u):
-        return h * len(units) + u
+        size = slots[h] if u == home(h) else size
+        arrived(ybuf.at[y, pl.ds(start, size), :], x_r.at[index(h, u)])
 
     def spread(h, u):
         x_wait(h, u)
@@ -265,32 +286,33 @@
         experts(*span(h, u))
 
     def compute_home():
-        for h in (0, 1):
-            y_wait(h, last)
-        experts(0, 2 * both)
-        for h in (0, 1):
+        for h in range(len(parts)):
+            y_wait(h, home(h))
+        experts(0, home_rows)
+        for h in range(len(parts)):
             other = 1 - c
             send(
-                obuf.at[:, rows(base(h, 0, other), slots), :],
-                rbuf0.at[:, rows(base(h, 0, c), slots), :],
-                home_s, b_r.at[index(h, last)], dev(x, y, z, other),
+                obuf.at[:, rows(base(h, 0, other), slots[h]), :],
+                rbuf0.at[:, rows(base(h, 0, c), slots[h]), :],
+                home_s, b_r.at[index(h, home(h))], dev(x, y, z, other),
             )
-            here = rows(base(h, 0, c), slots)
+            here = rows(base(h, 0, c), slots[h])
             for q in range(ny):
                 rbuf0[q, here, :] = obuf[q, here, :]
 
     def combine_home():
-        for h in (0, 1):
-            arrived(rbuf0.at[:, pl.ds(base(h, 0, 0), slots), :], b_r.at[index(h, last)])
-            here = pl.ds(base(h, 0, 0), both)
+        for h in range(len(parts)):
+            arrived(rbuf0.at[:, pl.ds(base(h, 0, 0), slots[h]), :], b_r.at[index(h, home(h))])
+            here = pl.ds(base(h, 0, 0), both[h])
+            first, col = tokens_of(h)
             for o in range(ny):
                 term = lax.dot_general(
-                    swbuf[here, :], rbuf0[at_y(o), here, :], across, preferred_element_type=F32
+                    swbuf[here, 0:col], rbuf0[at_y(o), here, :], across, preferred_element_type=F32
                 )
                 if o == 0:
-                    part[h * col : (h + 1) * col, :] = term
+                    part[first : first + col, :] = term
                 else:
-                    part0[h * col : (h + 1) * col, (o - 1) * quarter : o * quarter] = term
+                    part0[first : first + col, (o - 1) * quarter : o * quarter] = term
 
     def give_one(h, u):
         start, size = span(h, u)
@@ -320,19 +342,20 @@
         arrived(r2buf.at[:, here, :], p2_r.at[index(h, u)])
         total = obuf[y, here, :].astype(F32) + r2buf[0, here, :].astype(F32)
         xret[here, :] = (total + r2buf[1, here, :].astype(F32)).astype(BF16)
-        for g in units[u]:
-            land = rbuf.at[rows(base(h, g, c), slots), :]
+        for g in units[h][u]:
+            land = rbuf.at[rows(base(h, g, c), slots[h]), :]
             for c_ in range(nc):
                 send(
-                    xret.at[pl.ds(base(h, g, c_), slots), :], land, b_s,
+                    xret.at[pl.ds(base(h, g, c_), slots[h]), :], land, b_s,
                     b_r.at[index(h, u)], dev(from_x(g), y, z, c_),
                 )
 
     def combine(h, u):
         here = pl.ds(*span(h, u))
+        first, col = tokens_of(h)
         arrived(rbuf.at[here, :], b_r.at[index(h, u)])
-        part[h * col : (h + 1) * col, :] += lax.dot_general(
-            swbuf[here, :], rbuf[here, :], across, preferred_element_type=F32
+        part[first : first + col, :] += lax.dot_general(
+            swbuf[here, 0:col], rbuf[here, :], across, preferred_element_type=F32
         )
 
     reach = nz // 2
@@ -372,89 +395,90 @@
     own_hop, next_hop, finish = reducer(part, zs, zr, zrs_s, zrs_r)
     wide_own, wide_next, wide_finish = reducer(part0, ws, wr, wrs_s, wrs_r)
 
-    near, far = 0, 1
-    rest = tuple(range(1, last))
-
     def wide_step(k):
         if k < steps:
             wide_next(k)
             wide_own(k + 1)
 
+    def choose(h):
+        rank, weight = routes(h)
+        for g in range(nx):
+            select(h, g, rank, weight)
+
+    near, between = 0, range(1, far)
+    outer = range(len(units[far]) - 1)
     for d in (1, -1):
         gather_send(1, d)
-    for k in range(1, mid + 1):
+    gather_step(1)
+    gather_rest(near)
+    choose(near)
+    spread(near, home(near))
+    for h in between:
+        gather_step(h + 1)
+    spread(near, 0)
+    forward(near, home(near))
+    for h in between:
+        gather_rest(h)
+        choose(h)
+        spread(h, home(h))
+    for k in range(far + 1, steps):
         gather_step(k)
-    gather_rest(near)
-    rank, weight = routes(near)
-    for g in range(nx):
-        select(near, g, rank, weight)
-    spread(near, last)
-    for k in range(mid + 1, steps):
-        gather_step(k)
-    spread(near, 0)
-    forward(near, last)
+    forward(near, 0)
+    for h in between:
+        spread(h, 0)
+        forward(h, home(h))
     gather_step(steps)
     gather_rest(far)
-    rank, weight = routes(far)
-    for g in range(nx):
-        select(far, g, rank, weight)
-    spread(far, last)
-    for u in rest:
-        spread(near, u)
-    forward(near, 0)
-    forward(far, last)
-    spread(far, 0)
-    for u in rest:
-        forward(near, u)
+    choose(far)
+    spread(far, home(far))
+    for h in between:
+        forward(h, 0)
+    forward(far, home(far))
+    for u in outer:
         spread(far, u)
     for load in loads:
         load.wait()
+    for h in range(far):
+        compute(h, 0)
     compute_home()
-    compute(near, 0)
-    give_one(near, 0)
+    forward(far, 0)
     combine_home()
     wide_own(1)
-    forward(far, 0)
-    for u in rest:
-        compute(near, u)
-        give_one(near, u)
+    for u in outer[1:]:
         forward(far, u)
-    wide_step(1)
-    for u in rest:
-        give_two(near, u)
-    compute(far, 0)
-    give_one(far, 0)
-    for u in rest:
+    for h in range(far - 1, -1, -1):
+        give_one(h, 0)
+    for u in outer:
         compute(far, u)
         give_one(far, u)
+    wide_step(1)
+    for u in outer:
+        give_two(far, u)
+    for h in range(far - 1, -1, -1):
+        give_two(h, 0)
     wide_step(2)
-    give_two(far, 0)
-    for u in rest:
-        give_two(far, u)
-    give_two(near, 0)
+    give_back(far, 0)
     for k in range(3, steps):
         wide_step(k)
-    for u in rest:
-        give_back(near, u)
-    give_back(far, 0)
-    for u in rest:
+    for u in outer[1:]:
         give_back(far, u)
-    for u in range(last):
+    for h in between:
+        give_back(h, 0)
+    for u in outer:
         combine(far, u)
     for k in range(1, mid + 1):
         own_hop(k)
-    wide = wide_finish()
+    give_back(near, 0)
     for k in range(1, mid):
         next_hop(k)
-    give_back(near, 0)
-    for u in rest:
-        combine(near, u)
+    wide = wide_finish()
+    for h in between:
+        combine(h, 0)
+        next_hop(mid)
+        own_hop(mid + 1)
     combine(near, 0)
-    next_hop(mid)
-    for k in range(mid + 1, steps + 1):
-        own_hop(k)
-    for k in range(mid + 1, steps):
-        next_hop(k)
+    own_hop(steps)
+    next_hop(steps - 1)
     main = finish()
 
     count = out_ref.shape[0]
@@ -473,16 +497,17 @@
     out_ref[...] = total.astype(BF16)
 
     every = ybuf.shape[1]
-    moved = every - 2 * both
+    moved = every - home_rows
+    sent = sum(slots)
     for sem, ref in (
         (zag_s, zbuf.at[pl.ds(0, (nz - 1) * tile), :]),
-        (x_s, xsend.at[pl.ds(0, 2 * (nx * nc - 1) * slots), :]),
+        (x_s, xsend.at[pl.ds(0, (nx * nc - 1) * sent), :]),
         (y1_s, ybuf.at[pl.ds(0, 2), :, :]),
         (y2_s, ybuf.at[0]),
         (p1_s, ybuf.at[0, pl.ds(0, moved), :]),
         (p2_s, r2buf.at[:, pl.ds(0, moved), :]),
         (b_s, xret.at[pl.ds(0, moved), :]),
-        (home_s, rbuf0.at[:, pl.ds(0, 2 * slots), :]),
+        (home_s, rbuf0.at[:, pl.ds(0, sent), :]),
         (zrs_s, ybuf.at[0, pl.ds(0, (nz - 1) * tile), :]),
         (wrs_s, part0.at[pl.ds(0, (nz - 1) * tile // 2), :]),
         (f_s, fsend.at[pl.ds(0, ny - 1)]),
@@ -504,7 +529,7 @@
     vmem = pl.BlockSpec(memory_space=pltpu.VMEM)
     hbm = pl.BlockSpec(memory_space=pl.ANY)
     flops = 6 * every * width * hidden
-    units = 2 * (nx // 2 + 1)
+    units = 7
     home = 2 * nc * slots // 2
     return pl.pallas_call(
         functools.partial(kernel, nx, nz),
@@ -535,7 +560,7 @@
             pltpu.VMEM((ny, tile // ny, width), BF16),
             dma((4,)),
             dma((11,)),
-            dma((2 * steps,)), dma((2,)),
+            dma((2 * steps,)), dma((3,)),
             dma((units,)), dma((units,)), dma((units,)), dma((units,)), dma((units,)), dma((units,)),
             dma((2 * steps,)), dma((2 * steps,)), dma((1,)),
         ],

time: 106 us -> 101 us (0.953); the launches traced: 105 us -> 99.4 us
  Pallas kernels: 104 us -> 98 us
    pallas_call x1, Pallas kernels: 104 us -> 98 us  [on_device(): pl.pallas_call(functools.partial(kernel, nx, nz), out_shape=jax.ShapeDtyp...]
where the time goes in v5:
time: 101 us; the launch traced here: 99.4 us
  Pallas kernels  98 us (97%)
  local copies, waits for them, and re-layouts  1.37 us (1%)
    pallas_call x1, Pallas kernels, on_device(): pl.pallas_call(functools.partial(kernel, nx, nz), out_shape=jax.ShapeDtyp...  98 us

profile of v5, /device:TPU:1, one launch (start us, length us, event | category | flops | bytes accessed | tf_op | source)
XLA Modules:
  0.0 99.4 jit_solution(3987143898299258859)
XLA Ops:
  0.0 98.0 %shard_map.64 = bf16[4,3584]{1,0:T(4,128)(2,1)} custom-call(s32[8,16]{1,0:T(8,128)} %bitcast.2, f32[8,16]{1,0:T(8,128)} %bitcast.3, bf16[16,3584]{1,0:T(8,128)(2,1)} %tok_hbm.1, bf16[1,3584,256]{2,1,0:T(8,128)(2,1)} %wg_hbm.1, bf16[1,3584,256]{2,1,0:T(8,128)(2,1)} %wu_hbm.1, bf16[1,256,3584]{2,1,0:T(8,128)(2,1)} %wd_hbm.1), custom_call_target="tpu_custom_call" | custom-call | flops 2818572288 | bytes 8388608 | tf_op jit(solution)/shard_map/pallas_call | solution.py:534
  98.0 1.4 %copy.8 = bf16[4,3584]{1,0:T(4,128)(2,1)} copy(bf16[4,3584]{1,0:T(4,128)(2,1)} %shard_map.64) | data formatting | bytes 57344

commit v6 on v5

--- a/solution.py
+++ b/solution.py
@@ -18,10 +18,10 @@
 
 
 def kernel(
-    nx, nz, ids_ref, logits_ref, tok_hbm, wg_hbm, wu_hbm, wd_hbm, out_ref,
-    wg, wu, wd, zbuf, swbuf, xsend, ybuf, obuf, r1buf, r2buf, xret, rbuf, rbuf0, part, part0,
-    zs, zr, ws, wr, fsend, frecv,
-    w_sem, s_sem, zag_r, zag_one, x_r, y1_r, y2_r, p1_r, p2_r, b_r, zrs_r, wrs_r, f_r,
+    nx, nz, ids_hbm, logits_hbm, tok_hbm, wg_hbm, wu_hbm, wd_hbm, out_ref,
+    ids_ref, logits_ref, wg, wu, wd, zbuf, swbuf, xsend, ybuf, obuf, r1buf, r2buf, xret, rbuf, rbuf0, part, part0,
+    zs, zr, ws, wr, ds, dr, fsend, frecv,
+    w_sem, s_sem, zag_r, zag_one, x_r, y1_r, y2_r, p1_r, p2_r, b_r, zrs_r, wrs_r, f_r, d_r,
 ):
     nc, ny = CORES, N_DP
     tile, width = tok_hbm.shape
@@ -41,15 +41,15 @@
     home_rows = sum(both)
     offsets = {2: (0, 1), 4: (0, 1, 3, 2)}[nx]
     units = [
-        {2: ((1,), (0,)), 4: ((1, 2, 3), (0,)) if h < far else ((3,), (1, 2), (0,))}[nx]
+        {2: ((1,), (0,)), 4: ((1, 2, 3), (0,)) if h < far else ((1, 2), (3,), (0,))}[nx]
         for h in range(len(parts))
     ]
     unit_index = {}
     for h in range(len(parts)):
         for u in range(len(units[h])):
             unit_index[h, u] = len(unit_index)
-    (zag_s, x_s, y1_s, y2_s, p1_s, p2_s, b_s, home_s, zrs_s, wrs_s, f_s) = [
-        s_sem.at[i] for i in range(11)
+    (zag_s, x_s, y1_s, y2_s, p1_s, p2_s, b_s, home_s, zrs_s, wrs_s, f_s, d_s) = [
+        s_sem.at[i] for i in range(12)
     ]
     ep = lax.axis_index("ep")
     y = lax.axis_index("dp")
@@ -115,7 +115,7 @@
         awaits(ref, sem).wait_recv()
 
     barrier = pltpu.get_barrier_semaphore()
-    peers = [dev(x, y, at_z(o), c) for o in (1, -1, 2, -2)]
+    peers = [dev(x, y, at_z(o * d), c) for o in range(1, nz // 4 + 1) for d in (1, -1)]
     peers += [dev(from_x(g), y, z, c_) for g in range(1, nx) for c_ in range(nc)]
     peers += [dev(x, y, z, 1 - c)]
     peers += [dev(x, at_y(o), z, c) for o in range(1, ny)]
@@ -127,7 +127,15 @@
         tok_hbm.at[:, pl.ds(pl.multiple_of(y * quarter, 128), quarter)],
         zbuf.at[own, pl.ds(0, quarter)], w_sem.at[3],
     )
+    names = [
+        pltpu.make_async_copy(ids_hbm, ids_ref, w_sem.at[4]),
+        pltpu.make_async_copy(logits_hbm, logits_ref, w_sem.at[5]),
+    ]
+    for copy in names:
+        copy.start()
     mine.start()
+    for copy in names:
+        copy.wait()
     scores = 1.0 / (1.0 + jnp.exp(-logits_ref[...]))
     wts = ROUTE_SCALE * scores / jnp.sum(scores, axis=0, keepdims=True)
     lane = lax.broadcasted_iota(jnp.int32, (top, 128), 1)
@@ -390,10 +398,10 @@
         def finish():
             return block_of(0) + zget(1, steps) + zget(-1, steps)
 
-        return own_hop, next_hop, finish
-
-    own_hop, next_hop, finish = reducer(part, zs, zr, zrs_s, zrs_r)
-    wide_own, wide_next, wide_finish = reducer(part0, ws, wr, wrs_s, wrs_r)
+        return own_hop, next_hop, finish, block_of, zget
+
+    own_hop, next_hop, _, block_of, zget = reducer(part, zs, zr, zrs_s, zrs_r)
+    wide_own, wide_next, wide_finish, _, _ = reducer(part0, ws, wr, wrs_s, wrs_r)
 
     def wide_step(k):
         if k < steps:
@@ -404,6 +412,23 @@
         rank, weight = routes(h)
         for g in range(nx):
             select(h, g, rank, weight)
+
+    direct = nz // 4
+
+    def straight(o):
+        value = block_of(o)
+        if abs(o) == direct:
+            value = value + zget(1 if o > 0 else -1, mid)
+        n = (o if o > 0 else direct - o) - 1
+        ds[n] = value.astype(BF16)
+        send(ds.at[n], dr.at[n], d_s, d_r.at[0], dev(x, y, at_z(o), c))
+
+    def gathered():
+        arrived(dr, d_r.at[0])
+        total = block_of(0)
+        for n in range(2 * direct):
+            total += dr[n].astype(F32)
+        return total
 
     near, between = 0, range(1, far)
     outer = range(len(units[far]) - 1)
@@ -416,25 +441,27 @@
     for h in between:
         gather_step(h + 1)
     spread(near, 0)
-    forward(near, home(near))
     for h in between:
         gather_rest(h)
         choose(h)
         spread(h, home(h))
+    forward(near, home(near))
     for k in range(far + 1, steps):
         gather_step(k)
-    forward(near, 0)
     for h in between:
         spread(h, 0)
-        forward(h, home(h))
     gather_step(steps)
     gather_rest(far)
     choose(far)
     spread(far, home(far))
+    forward(near, 0)
+    for h in between:
+        forward(h, home(h))
+    spread(far, 0)
     for h in between:
         forward(h, 0)
     forward(far, home(far))
-    for u in outer:
+    for u in outer[1:]:
         spread(far, u)
     for load in loads:
         load.wait()
@@ -446,22 +473,22 @@
     wide_own(1)
     for u in outer[1:]:
         forward(far, u)
-    for h in range(far - 1, -1, -1):
+    for h in between:
         give_one(h, 0)
     for u in outer:
         compute(far, u)
         give_one(far, u)
+    give_one(near, 0)
     wide_step(1)
     for u in outer:
         give_two(far, u)
     for h in range(far - 1, -1, -1):
         give_two(h, 0)
     wide_step(2)
-    give_back(far, 0)
+    for u in outer:
+        give_back(far, u)
     for k in range(3, steps):
         wide_step(k)
-    for u in outer[1:]:
-        give_back(far, u)
     for h in between:
         give_back(h, 0)
     for u in outer:
@@ -471,15 +498,18 @@
     give_back(near, 0)
     for k in range(1, mid):
         next_hop(k)
+    for h in between:
+        combine(h, 0)
+        for o in (3, -3, 2):
+            straight(o)
     wide = wide_finish()
-    for h in between:
-        combine(h, 0)
-        next_hop(mid)
-        own_hop(mid + 1)
     combine(near, 0)
-    own_hop(steps)
-    next_hop(steps - 1)
-    main = finish()
+    for o in range(2 if nz > 8 else 1, 0, -1):
+        straight(-o)
+    straight(1)
+    for o in (direct, -direct):
+        straight(o)
+    main = gathered()
 
     count = out_ref.shape[0]
     for o in range(ny):
@@ -508,7 +538,8 @@
         (p2_s, r2buf.at[:, pl.ds(0, moved), :]),
         (b_s, xret.at[pl.ds(0, moved), :]),
         (home_s, rbuf0.at[:, pl.ds(0, sent), :]),
-        (zrs_s, ybuf.at[0, pl.ds(0, (nz - 1) * tile), :]),
+        (zrs_s, ybuf.at[0, pl.ds(0, (4 * mid - 1) * tile), :]),
+        (d_s, ds),
         (wrs_s, part0.at[pl.ds(0, (nz - 1) * tile // 2), :]),
         (f_s, fsend.at[pl.ds(0, ny - 1)]),
     ):
@@ -534,9 +565,11 @@
     return pl.pallas_call(
         functools.partial(kernel, nx, nz),
         out_shape=jax.ShapeDtypeStruct((tile // ny, width), BF16),
-        in_specs=[vmem, vmem, hbm, hbm, hbm, hbm],
+        in_specs=[hbm] * 6,
         out_specs=vmem,
         scratch_shapes=[
+            pltpu.VMEM(expert_ids.shape[::-1], jnp.int32),
+            pltpu.VMEM(expert_ids.shape[::-1], F32),
             pltpu.VMEM((width, hidden), BF16),
             pltpu.VMEM((width, hidden), BF16),
             pltpu.VMEM((hidden, width), BF16),
@@ -556,13 +589,15 @@
             pltpu.VMEM((2 * steps, 2, tile, quarter), BF16),
             pltpu.VMEM((2 * steps, 2, tile, width - quarter), BF16),
             pltpu.VMEM((2 * steps, 2, tile, width - quarter), BF16),
+            pltpu.VMEM((2 * steps, tile, quarter), BF16),
+            pltpu.VMEM((2 * steps, tile, quarter), BF16),
             pltpu.VMEM((ny, tile // ny, width), BF16),
             pltpu.VMEM((ny, tile // ny, width), BF16),
-            dma((4,)),
-            dma((11,)),
+            dma((6,)),
+            dma((12,)),
             dma((2 * steps,)), dma((3,)),
             dma((units,)), dma((units,)), dma((units,)), dma((units,)), dma((units,)), dma((units,)),
-            dma((2 * steps,)), dma((2 * steps,)), dma((1,)),
+            dma((2 * steps,)), dma((2 * steps,)), dma((1,)), dma((1,)),
         ],
         compiler_params=pltpu.CompilerParams(
             collective_id=0, has_side_effects=True, vmem_limit_bytes=56 * 1024 * 1024

time: 101 us -> 101 us (level)
  no operation moved by 1% of the time
where the time goes in v6:
time: 101 us; the launch traced here: 100 us
  Pallas kernels  99 us (98%)
  local copies, waits for them, and re-layouts  1.37 us (1%)
    pallas_call x1, Pallas kernels, on_device(): pl.pallas_call(functools.partial(kernel, nx, nz), out_shape=jax.ShapeDtyp...  99 us

profile of v6, /device:TPU:1, one launch (start us, length us, event | category | flops | bytes accessed | tf_op | source)
XLA Modules:
  0.0 100.3 jit_solution(4495837218217950837)
XLA Ops:
  0.0 99.0 %shard_map.64 = bf16[4,3584]{1,0:T(4,128)(2,1)} custom-call(s32[8,16]{1,0:T(8,128)} %bitcast.2, f32[8,16]{1,0:T(8,128)} %bitcast.3, bf16[16,3584]{1,0:T(8,128)(2,1)} %tok_hbm.1, bf16[1,3584,256]{2,1,0:T(8,128)(2,1)} %wg_hbm.1, bf16[1,3584,256]{2,1,0:T(8,128)(2,1)} %wu_hbm.1, bf16[1,256,3584]{2,1,0:T(8,128)(2,1)} %wd_hbm.1), custom_call_target="tpu_custom_call" | custom-call | flops 2818572288 | bytes 8388608 | tf_op jit(solution)/shard_map/pallas_call | solution.py:565
  99.0 1.4 %copy.8 = bf16[4,3584]{1,0:T(4,128)(2,1)} copy(bf16[4,3584]{1,0:T(4,128)(2,1)} %shard_map.64) | data formatting | bytes 57344

commit v7 on v6

--- a/solution.py
+++ b/solution.py
@@ -410,7 +410,8 @@
 
     def choose(h):
         rank, weight = routes(h)
-        for g in range(nx):
+        turns = (0, 3, 1, 2) if nx == 4 and h < far else range(nx)
+        for g in turns:
             select(h, g, rank, weight)
 
     direct = nz // 4
@@ -440,10 +441,10 @@
     spread(near, home(near))
     for h in between:
         gather_step(h + 1)
-    spread(near, 0)
-    for h in between:
         gather_rest(h)
         choose(h)
+    spread(near, 0)
+    for h in between:
         spread(h, home(h))
     forward(near, home(near))
     for k in range(far + 1, steps):
@@ -453,15 +454,14 @@
     gather_step(steps)
     gather_rest(far)
     choose(far)
+    for h in between:
+        forward(h, home(h))
+    forward(near, 0)
     spread(far, home(far))
-    forward(near, 0)
-    for h in between:
-        forward(h, home(h))
-    spread(far, 0)
     for h in between:
         forward(h, 0)
     forward(far, home(far))
-    for u in outer[1:]:
+    for u in outer:
         spread(far, u)
     for load in loads:
         load.wait()

time: 101 us -> 99.9 us (0.989)
  no operation moved by 1% of the time
where the time goes in v7:
time: 99.9 us; the launch traced here: 99.7 us
  Pallas kernels  98.3 us (98%)
  local copies, waits for them, and re-layouts  1.37 us (1%)
    pallas_call x1, Pallas kernels, on_device(): pl.pallas_call(functools.partial(kernel, nx, nz), out_shape=jax.ShapeDtyp...  98.3 us

profile of v7, /device:TPU:1, one launch (start us, length us, event | category | flops | bytes accessed | tf_op | source)
XLA Modules:
  0.0 99.7 jit_solution(15889412392279225187)
XLA Ops:
  0.0 98.3 %shard_map.64 = bf16[4,3584]{1,0:T(4,128)(2,1)} custom-call(s32[8,16]{1,0:T(8,128)} %bitcast.2, f32[8,16]{1,0:T(8,128)} %bitcast.3, bf16[16,3584]{1,0:T(8,128)(2,1)} %tok_hbm.1, bf16[1,3584,256]{2,1,0:T(8,128)(2,1)} %wg_hbm.1, bf16[1,3584,256]{2,1,0:T(8,128)(2,1)} %wu_hbm.1, bf16[1,256,3584]{2,1,0:T(8,128)(2,1)} %wd_hbm.1), custom_call_target="tpu_custom_call" | custom-call | flops 2818572288 | bytes 8388608 | tf_op jit(solution)/shard_map/pallas_call | solution.py:565
  98.3 1.4 %copy.8 = bf16[4,3584]{1,0:T(4,128)(2,1)} copy(bf16[4,3584]{1,0:T(4,128)(2,1)} %shard_map.64) | data formatting | bytes 57344

commit v8 on v7

--- a/solution.py
+++ b/solution.py
@@ -48,8 +48,8 @@
     for h in range(len(parts)):
         for u in range(len(units[h])):
             unit_index[h, u] = len(unit_index)
-    (zag_s, x_s, y1_s, y2_s, p1_s, p2_s, b_s, home_s, zrs_s, wrs_s, f_s, d_s) = [
-        s_sem.at[i] for i in range(12)
+    (zag_s, x_s, y1_s, y2_s, p1_s, p2_s, b_s, home_s, zrs_s, wrs_s, f_s, d_s, o_s) = [
+        s_sem.at[i] for i in range(13)
     ]
     ep = lax.axis_index("ep")
     y = lax.axis_index("dp")
@@ -115,7 +115,7 @@
         awaits(ref, sem).wait_recv()
 
     barrier = pltpu.get_barrier_semaphore()
-    peers = [dev(x, y, at_z(o * d), c) for o in range(1, nz // 4 + 1) for d in (1, -1)]
+    peers = [dev(x, y, at_z(o), c) for o in (1, -1, 2, -2)]
     peers += [dev(from_x(g), y, z, c_) for g in range(1, nx) for c_ in range(nc)]
     peers += [dev(x, y, z, 1 - c)]
     peers += [dev(x, at_y(o), z, c) for o in range(1, ny)]
@@ -416,20 +416,41 @@
 
     direct = nz // 4
 
+    count = out_ref.shape[0]
+
     def straight(o):
         value = block_of(o)
         if abs(o) == direct:
             value = value + zget(1 if o > 0 else -1, mid)
-        n = (o if o > 0 else direct - o) - 1
-        ds[n] = value.astype(BF16)
-        send(ds.at[n], dr.at[n], d_s, d_r.at[0], dev(x, y, at_z(o), c))
-
-    def gathered():
-        arrived(dr, d_r.at[0])
-        total = block_of(0)
+        n = (o if o > 0 else direct - o) - 1 if o else 2 * direct
+        for q in range(ny):
+            ds[n, q] = value[q * count : (q + 1) * count, :].astype(BF16)
+        for r in range(ny) if o else range(1, ny):
+            send(
+                ds.at[n, at_y(r)], dr.at[y, n], d_s if o else o_s, d_r.at[0 if o else 1],
+                dev(x, at_y(r), at_z(o), c),
+            )
+        if o == 0:
+            dr[y, n] = ds[n, y]
+
+    def share_wide():
+        wide = wide_finish()
+        for q in range(ny):
+            fsend[q] = wide[q * count : (q + 1) * count, :].astype(BF16)
+        for r in (2, 1, 3):
+            send(fsend.at[at_y(r)], frecv.at[y], f_s, f_r.at[0], dev(x, at_y(r), z, c))
+        frecv[y] = fsend[y]
+
+    def gathered(j):
+        where = at_y(j)
+        total = dr[where, 2 * direct].astype(F32)
+        for r in range(ny):
+            o = (j - r) % ny
+            if o:
+                total += frecv[at_y(r), :, (o - 1) * quarter : o * quarter].astype(F32)
         for n in range(2 * direct):
-            total += dr[n].astype(F32)
-        return total
+            total += dr[where, n].astype(F32)
+        return total.astype(BF16)
 
     near, between = 0, range(1, far)
     outer = range(len(units[far]) - 1)
@@ -441,10 +462,10 @@
     spread(near, home(near))
     for h in between:
         gather_step(h + 1)
+    spread(near, 0)
+    for h in between:
         gather_rest(h)
         choose(h)
-    spread(near, 0)
-    for h in between:
         spread(h, home(h))
     forward(near, home(near))
     for k in range(far + 1, steps):
@@ -454,11 +475,10 @@
     gather_step(steps)
     gather_rest(far)
     choose(far)
-    for h in between:
-        forward(h, home(h))
     forward(near, 0)
     spread(far, home(far))
     for h in between:
+        forward(h, home(h))
         forward(h, 0)
     forward(far, home(far))
     for u in outer:
@@ -502,29 +522,20 @@
         combine(h, 0)
         for o in (3, -3, 2):
             straight(o)
-    wide = wide_finish()
+    share_wide()
     combine(near, 0)
     for o in range(2 if nz > 8 else 1, 0, -1):
         straight(-o)
     straight(1)
+    straight(0)
     for o in (direct, -direct):
         straight(o)
-    main = gathered()
-
-    count = out_ref.shape[0]
-    for o in range(ny):
-        share = (main if o == 0 else wide[:, (o - 1) * quarter : o * quarter]).astype(BF16)
-        piece = pl.ds(pl.multiple_of(at_y(o) * quarter, 128), quarter)
-        for n in range(ny):
-            fsend[n, :, piece] = share[n * count : (n + 1) * count, :]
-    for o in (2, 1, 3):
-        send(fsend.at[at_y(o)], frecv.at[y], f_s, f_r.at[0], dev(x, at_y(o), z, c))
-    frecv[y] = fsend[y]
     arrived(frecv.at[pl.ds(0, ny - 1)], f_r.at[0])
-    total = frecv[0].astype(F32)
-    for q in range(1, ny):
-        total += frecv[q].astype(F32)
-    out_ref[...] = total.astype(BF16)
+    arrived(dr.at[pl.ds(0, ny - 1), 2 * direct], d_r.at[1])
+    arrived(dr.at[:, pl.ds(0, 2 * direct)], d_r.at[0])
+    for j in range(ny):
+        piece = pl.ds(pl.multiple_of(at_y(j) * quarter, 128), quarter)
+        out_ref[:, piece] = gathered(j)
 
     every = ybuf.shape[1]
     moved = every - home_rows
@@ -539,7 +550,8 @@
         (b_s, xret.at[pl.ds(0, moved), :]),
         (home_s, rbuf0.at[:, pl.ds(0, sent), :]),
         (zrs_s, ybuf.at[0, pl.ds(0, (4 * mid - 1) * tile), :]),
-        (d_s, ds),
+        (d_s, ds.at[pl.ds(0, 2 * direct)]),
+        (o_s, ds.at[0, pl.ds(0, ny - 1)]),
         (wrs_s, part0.at[pl.ds(0, (nz - 1) * tile // 2), :]),
         (f_s, fsend.at[pl.ds(0, ny - 1)]),
     ):
@@ -589,15 +601,15 @@
             pltpu.VMEM((2 * steps, 2, tile, quarter), BF16),
             pltpu.VMEM((2 * steps, 2, tile, width - quarter), BF16),
             pltpu.VMEM((2 * steps, 2, tile, width - quarter), BF16),
-            pltpu.VMEM((2 * steps, tile, quarter), BF16),
-            pltpu.VMEM((2 * steps, tile, quarter), BF16),
-            pltpu.VMEM((ny, tile // ny, width), BF16),
-            pltpu.VMEM((ny, tile // ny, width), BF16),
+            pltpu.VMEM((2 * steps + 1, ny, tile // ny, quarter), BF16),
+            pltpu.VMEM((ny, 2 * steps + 1, tile // ny, quarter), BF16),
+            pltpu.VMEM((ny, tile // ny, width - quarter), BF16),
+            pltpu.VMEM((ny, tile // ny, width - quarter), BF16),
             dma((6,)),
-            dma((12,)),
+            dma((13,)),
             dma((2 * steps,)), dma((3,)),
             dma((units,)), dma((units,)), dma((units,)), dma((units,)), dma((units,)), dma((units,)),
-            dma((2 * steps,)), dma((2 * steps,)), dma((1,)), dma((1,)),
+            dma((2 * steps,)), dma((2 * steps,)), dma((1,)), dma((2,)),
         ],
         compiler_params=pltpu.CompilerParams(
             collective_id=0, has_side_effects=True, vmem_limit_bytes=56 * 1024 * 1024

time: 99.9 us -> 95.9 us (0.960)
  Pallas kernels: 98.3 us -> 94.3 us
    pallas_call x1, Pallas kernels: 98.3 us -> 94.3 us  [on_device(): pl.pallas_call(functools.partial(kernel, nx, nz), out_shape=jax.ShapeDtyp...]
where the time goes in v8:
time: 95.9 us; the launch traced here: 95.7 us
  Pallas kernels  94.3 us (98%)
  local copies, waits for them, and re-layouts  1.37 us (1%)
    pallas_call x1, Pallas kernels, on_device(): pl.pallas_call(functools.partial(kernel, nx, nz), out_shape=jax.ShapeDtyp...  94.3 us

profile of v8, /device:TPU:1, one launch (start us, length us, event | category | flops | bytes accessed | tf_op | source)
XLA Modules:
  0.0 95.7 jit_solution(1752350798673261232)
XLA Ops:
  0.0 94.3 %shard_map.64 = bf16[4,3584]{1,0:T(4,128)(2,1)} custom-call(s32[8,16]{1,0:T(8,128)} %bitcast.2, f32[8,16]{1,0:T(8,128)} %bitcast.3, bf16[16,3584]{1,0:T(8,128)(2,1)} %tok_hbm.1, bf16[1,3584,256]{2,1,0:T(8,128)(2,1)} %wg_hbm.1, bf16[1,3584,256]{2,1,0:T(8,128)(2,1)} %wu_hbm.1, bf16[1,256,3584]{2,1,0:T(8,128)(2,1)} %wd_hbm.1), custom_call_target="tpu_custom_call" | custom-call | flops 2818572288 | bytes 8388608 | tf_op jit(solution)/shard_map/pallas_call | solution.py:577
  94.3 1.4 %copy.8 = bf16[4,3584]{1,0:T(4,128)(2,1)} copy(bf16[4,3584]{1,0:T(4,128)(2,1)} %shard_map.64) | data formatting | bytes 57344

commit v9 on v8

--- a/solution.py
+++ b/solution.py
@@ -41,7 +41,7 @@
     home_rows = sum(both)
     offsets = {2: (0, 1), 4: (0, 1, 3, 2)}[nx]
     units = [
-        {2: ((1,), (0,)), 4: ((1, 2, 3), (0,)) if h < far else ((1, 2), (3,), (0,))}[nx]
+        {2: ((1,), (0,)), 4: ((1, 2, 3), (0,)) if h < far else ((3,), (1, 2), (0,))}[nx]
         for h in range(len(parts))
     ]
     unit_index = {}
@@ -493,15 +493,16 @@
     wide_own(1)
     for u in outer[1:]:
         forward(far, u)
-    for h in between:
-        give_one(h, 0)
     for u in outer:
         compute(far, u)
         give_one(far, u)
-    give_one(near, 0)
+        if u == 0:
+            for h in between:
+                give_one(h, 0)
     wide_step(1)
     for u in outer:
         give_two(far, u)
+    give_one(near, 0)
     for h in range(far - 1, -1, -1):
         give_two(h, 0)
     wide_step(2)
@@ -509,15 +510,15 @@
         give_back(far, u)
     for k in range(3, steps):
         wide_step(k)
-    for h in between:
-        give_back(h, 0)
     for u in outer:
         combine(far, u)
     for k in range(1, mid + 1):
         own_hop(k)
-    give_back(near, 0)
+    for h in between:
+        give_back(h, 0)
     for k in range(1, mid):
         next_hop(k)
+    give_back(near, 0)
     for h in between:
         combine(h, 0)
         for o in (3, -3, 2):

time: 95.9 us -> 104 us (1.084)
  Pallas kernels: 94.3 us -> 102 us
    pallas_call x1, Pallas kernels: 94.3 us -> 102 us  [on_device(): pl.pallas_call(functools.partial(kernel, nx, nz), out_shape=jax.ShapeDtyp...]
where the time goes in v9:
time: 104 us; the launch traced here: 103 us
  Pallas kernels  102 us (98%)
  local copies, waits for them, and re-layouts  1.37 us (1%)
    pallas_call x1, Pallas kernels, on_device(): pl.pallas_call(functools.partial(kernel, nx, nz), out_shape=jax.ShapeDtyp...  102 us

profile of v9, /device:TPU:1, one launch (start us, length us, event | category | flops | bytes accessed | tf_op | source)
XLA Modules:
  0.0 103.5 jit_solution(4694151282230369248)
XLA Ops:
  0.0 102.1 %shard_map.64 = bf16[4,3584]{1,0:T(4,128)(2,1)} custom-call(s32[8,16]{1,0:T(8,128)} %bitcast.2, f32[8,16]{1,0:T(8,128)} %bitcast.3, bf16[16,3584]{1,0:T(8,128)(2,1)} %tok_hbm.1, bf16[1,3584,256]{2,1,0:T(8,128)(2,1)} %wg_hbm.1, bf16[1,3584,256]{2,1,0:T(8,128)(2,1)} %wu_hbm.1, bf16[1,256,3584]{2,1,0:T(8,128)(2,1)} %wd_hbm.1), custom_call_target="tpu_custom_call" | custom-call | flops 2818572288 | bytes 8388608 | tf_op jit(solution)/shard_map/pallas_call | solution.py:578
  102.1 1.4 %copy.8 = bf16[4,3584]{1,0:T(4,128)(2,1)} copy(bf16[4,3584]{1,0:T(4,128)(2,1)} %shard_map.64) | data formatting | bytes 57344

commit v10 on v9

--- a/solution.py
+++ b/solution.py
@@ -500,25 +500,29 @@
             for h in between:
                 give_one(h, 0)
     wide_step(1)
-    for u in outer:
+    give_two(far, 0)
+    give_one(near, 0)
+    for u in outer[1:]:
         give_two(far, u)
-    give_one(near, 0)
-    for h in range(far - 1, -1, -1):
+    for h in between:
         give_two(h, 0)
     wide_step(2)
-    for u in outer:
+    give_back(far, 0)
+    give_two(near, 0)
+    for u in outer[1:]:
         give_back(far, u)
     for k in range(3, steps):
         wide_step(k)
-    for u in outer:
+    combine(far, 0)
+    for h in between:
+        give_back(h, 0)
+    for u in outer[1:]:
         combine(far, u)
     for k in range(1, mid + 1):
         own_hop(k)
-    for h in between:
-        give_back(h, 0)
+    give_back(near, 0)
     for k in range(1, mid):
         next_hop(k)
-    give_back(near, 0)
     for h in between:
         combine(h, 0)
         for o in (3, -3, 2):

time: 104 us -> 96.6 us (0.929)
  Pallas kernels: 102 us -> 94.7 us
    pallas_call x1, Pallas kernels: 102 us -> 94.7 us  [on_device(): pl.pallas_call(functools.partial(kernel, nx, nz), out_shape=jax.ShapeDtyp...]
where the time goes in v10:
time: 96.6 us; the launch traced here: 96.1 us
  Pallas kernels  94.7 us (98%)
  local copies, waits for them, and re-layouts  1.37 us (1%)
    pallas_call x1, Pallas kernels, on_device(): pl.pallas_call(functools.partial(kernel, nx, nz), out_shape=jax.ShapeDtyp...  94.7 us

profile of v10, /device:TPU:1, one launch (start us, length us, event | category | flops | bytes accessed | tf_op | source)
XLA Modules:
  0.0 96.1 jit_solution(9734327791129526009)
XLA Ops:
  0.0 94.7 %shard_map.64 = bf16[4,3584]{1,0:T(4,128)(2,1)} custom-call(s32[8,16]{1,0:T(8,128)} %bitcast.2, f32[8,16]{1,0:T(8,128)} %bitcast.3, bf16[16,3584]{1,0:T(8,128)(2,1)} %tok_hbm.1, bf16[1,3584,256]{2,1,0:T(8,128)(2,1)} %wg_hbm.1, bf16[1,3584,256]{2,1,0:T(8,128)(2,1)} %wu_hbm.1, bf16[1,256,3584]{2,1,0:T(8,128)(2,1)} %wd_hbm.1), custom_call_target="tpu_custom_call" | custom-call | flops 2818572288 | bytes 8388608 | tf_op jit(solution)/shard_map/pallas_call | solution.py:582
  94.7 1.4 %copy.8 = bf16[4,3584]{1,0:T(4,128)(2,1)} copy(bf16[4,3584]{1,0:T(4,128)(2,1)} %shard_map.64) | data formatting | bytes 57344

commit v11 on v8

--- a/solution.py
+++ b/solution.py
@@ -41,8 +41,7 @@
     home_rows = sum(both)
     offsets = {2: (0, 1), 4: (0, 1, 3, 2)}[nx]
     units = [
-        {2: ((1,), (0,)), 4: ((1, 2, 3), (0,)) if h < far else ((1, 2), (3,), (0,))}[nx]
-        for h in range(len(parts))
+        {2: ((1,), (0,)), 4: ((1, 2), (3,), (0,))}[nx] for h in range(len(parts))
     ]
     unit_index = {}
     for h in range(len(parts)):
@@ -293,6 +292,12 @@
         y_wait(h, u)
         experts(*span(h, u))
 
+    def compute_all(h):
+        for u in range(home(h)):
+            y_wait(h, u)
+        start, _ = span(h, 0)
+        experts(start, (nx - 1) * both[h])
+
     def compute_home():
         for h in range(len(parts)):
             y_wait(h, home(h))
@@ -410,8 +415,7 @@
 
     def choose(h):
         rank, weight = routes(h)
-        turns = (0, 3, 1, 2) if nx == 4 and h < far else range(nx)
-        for g in turns:
+        for g in range(nx):
             select(h, g, rank, weight)
 
     direct = nz // 4
@@ -467,6 +471,8 @@
         gather_rest(h)
         choose(h)
         spread(h, home(h))
+    for u in outer[1:]:
+        spread(near, u)
     forward(near, home(near))
     for k in range(far + 1, steps):
         gather_step(k)
@@ -477,16 +483,23 @@
     choose(far)
     forward(near, 0)
     spread(far, home(far))
+    for u in outer[1:]:
+        forward(near, u)
+        for h in between:
+            spread(h, u)
     for h in between:
         forward(h, home(h))
         forward(h, 0)
     forward(far, home(far))
+    for u in outer[1:]:
+        for h in between:
+            forward(h, u)
     for u in outer:
         spread(far, u)
     for load in loads:
         load.wait()
     for h in range(far):
-        compute(h, 0)
+        compute_all(h)
     compute_home()
     forward(far, 0)
     combine_home()
@@ -494,36 +507,43 @@
     for u in outer[1:]:
         forward(far, u)
     for h in between:
-        give_one(h, 0)
+        for u in outer:
+            give_one(h, u)
     for u in outer:
         compute(far, u)
         give_one(far, u)
-    give_one(near, 0)
+    for u in outer:
+        give_one(near, u)
     wide_step(1)
     for u in outer:
         give_two(far, u)
     for h in range(far - 1, -1, -1):
-        give_two(h, 0)
+        for u in outer:
+            give_two(h, u)
     wide_step(2)
     for u in outer:
         give_back(far, u)
     for k in range(3, steps):
         wide_step(k)
     for h in between:
-        give_back(h, 0)
+        for u in outer:
+            give_back(h, u)
     for u in outer:
         combine(far, u)
     for k in range(1, mid + 1):
         own_hop(k)
-    give_back(near, 0)
+    for u in outer:
+        give_back(near, u)
     for k in range(1, mid):
         next_hop(k)
     for h in between:
-        combine(h, 0)
+        for u in outer:
+            combine(h, u)
         for o in (3, -3, 2):
             straight(o)
     share_wide()
-    combine(near, 0)
+    for u in outer:
+        combine(near, u)
     for o in range(2 if nz > 8 else 1, 0, -1):
         straight(-o)
     straight(1)
@@ -572,7 +592,7 @@
     vmem = pl.BlockSpec(memory_space=pltpu.VMEM)
     hbm = pl.BlockSpec(memory_space=pl.ANY)
     flops = 6 * every * width * hidden
-    units = 7
+    units = 9
     home = 2 * nc * slots // 2
     return pl.pallas_call(
         functools.partial(kernel, nx, nz),

time: 95.9 us -> 94.9 us (0.990)
  Pallas kernels: 94.3 us -> 93.3 us
    pallas_call x1, Pallas kernels: 94.3 us -> 93.3 us  [on_device(): pl.pallas_call(functools.partial(kernel, nx, nz), out_shape=jax.ShapeDtyp...]
where the time goes in v11:
time: 94.9 us; the launch traced here: 94.7 us
  Pallas kernels  93.3 us (98%)
  local copies, waits for them, and re-layouts  1.37 us (1%)
    pallas_call x1, Pallas kernels, on_device(): pl.pallas_call(functools.partial(kernel, nx, nz), out_shape=jax.ShapeDtyp...  93.3 us

profile of v11, /device:TPU:1, one launch (start us, length us, event | category | flops | bytes accessed | tf_op | source)
XLA Modules:
  0.0 94.7 jit_solution(3935197011712688132)
XLA Ops:
  0.0 93.3 %shard_map.64 = bf16[4,3584]{1,0:T(4,128)(2,1)} custom-call(s32[8,16]{1,0:T(8,128)} %bitcast.2, f32[8,16]{1,0:T(8,128)} %bitcast.3, bf16[16,3584]{1,0:T(8,128)(2,1)} %tok_hbm.1, bf16[1,3584,256]{2,1,0:T(8,128)(2,1)} %wg_hbm.1, bf16[1,3584,256]{2,1,0:T(8,128)(2,1)} %wu_hbm.1, bf16[1,256,3584]{2,1,0:T(8,128)(2,1)} %wd_hbm.1), custom_call_target="tpu_custom_call" | custom-call | flops 2818572288 | bytes 8388608 | tf_op jit(solution)/shard_map/pallas_call | solution.py:597
  93.3 1.4 %copy.8 = bf16[4,3584]{1,0:T(4,128)(2,1)} copy(bf16[4,3584]{1,0:T(4,128)(2,1)} %shard_map.64) | data formatting | bytes 57344
